TPU v7x, 128 devices: a whole 4x4x4 slice. The times are simulated.
128 devices in a mesh: group: 4 (over y_hi, core), patch: 32 (over y_lo, x, z).
Axes of the slice: x: 4, y: 4 (y_hi: 2, y_lo: 2; y = y_hi * 2 + y_lo), z: 4, core: 2. Of those that a mesh axis runs over, the one named last changes fastest.
Arguments:
- fine_nodes: bfloat16 [131072, 512], P(('group', 'patch')), may hold values from -6 to 6
- coarse_nodes: bfloat16 [2048, 512], P(('group', 'patch')), may hold values from -6 to 6
- fine_edges: bfloat16 [524288, 512], P(('group', 'patch')), may hold values from -6 to 6
- fine_senders: int32 [524288], P(('group', 'patch')), may hold values from 0 to 1279
- fine_receivers: int32 [524288], P(('group', 'patch')), may hold values from 0 to 1023
- fine_live: int32 [128], P(('group', 'patch')), may hold values from 128 to 4096, as said below
- up_edges: bfloat16 [65536, 512], P(('group', 'patch')), may hold values from -6 to 6
- up_senders: int32 [65536], P(('group', 'patch')), may hold values from 0 to 1023
- up_receivers: int32 [65536], P(('group', 'patch')), may hold values from 0 to 2047
- down_edges: bfloat16 [65536, 512], P(('group', 'patch')), may hold values from -6 to 6
- down_senders: int32 [65536], P(('group', 'patch')), may hold values from 0 to 2047
- down_receivers: int32 [65536], P(('group', 'patch')), may hold values from 0 to 1023
- edge_in_weight: bfloat16 [1536, 512], replicated, may hold values from -0.15625 to 0.15625
- edge_in_bias: float32 [512], replicated, may hold values from -3 to 3
- edge_out_weight: bfloat16 [512, 512], replicated, may hold values from -0.25 to 0.25
- edge_out_bias: float32 [512], replicated, may hold values from -3 to 3
- edge_gain: float32 [512], replicated, may hold values from 0.25 to 1.75
- edge_shift: float32 [512], replicated, may hold values from -2 to 2
- node_in_weight: bfloat16 [1024, 512], replicated, may hold values from -0.1875 to 0.1875
- node_in_bias: float32 [512], replicated, may hold values from -3 to 3
- node_out_weight: bfloat16 [512, 512], replicated, may hold values from -0.25 to 0.25
- node_out_bias: float32 [512], replicated, may hold values from -3 to 3
- node_gain: float32 [512], replicated, may hold values from 0.25 to 1.75
- node_shift: float32 [512], replicated, may hold values from -2 to 2
Outputs:
- fine_out: bfloat16 [131072, 512], P(('group', 'patch'))
- coarse_out: bfloat16 [2048, 512], P(('group', 'patch'))
- fine_edges_out: bfloat16 [524288, 512], P(('group', 'patch'))
- up_edges_out: bfloat16 [65536, 512], P(('group', 'patch'))
- down_edges_out: bfloat16 [65536, 512], P(('group', 'patch'))
Inputs may be any that keep to these rules, and one draw needn't show every extreme that they name: `fine_live`: a multiple of 128; some patch has all 4096 slots live in every draw.
All inputs are finite; a program needn't handle non-finite values.
Results may differ from a plain program's by a relative error of at most 0.0049.
Values may be sent and summed in bfloat16 or wider, within the bound.
A program may use at most 128 MiB of HBM per device.

v0:
```python
import jax
import jax.numpy as jnp
from jax import lax
from jax.sharding import PartitionSpec as P

RIM = 128


def extended(shard, sides, width):
    for axis, dim in sides:
        size, length = (lax.axis_size(axis), shard.shape[dim])
        up = [(i, (i + 1) % size) for i in range(size)]
        down = [(j, i) for i, j in up]
        last = lax.slice_in_dim(shard, length - width, length, axis=dim)
        first = lax.slice_in_dim(shard, 0, width, axis=dim)
        before = lax.ppermute(last, axis, up)
        after = lax.ppermute(first, axis, down)
        shard = jnp.concatenate([before, shard, after], axis=dim)
    return shard


def split_up(shard, dim, size):
    lengths = shard.shape
    parts = shard.reshape(*lengths[:dim], size, lengths[dim] // size, *lengths[dim + 1 :])
    return jnp.moveaxis(parts, dim, 0)


def sent_and_summed(shard, axis, dim):
    size = lax.axis_size(axis)
    parts = lax.all_to_all(split_up(shard, dim, size), axis, 0, 0, tiled=True)
    return jnp.sum(parts, axis=0)


def perceptron(inputs, in_weight, in_bias, out_weight, out_bias, gain, shift):
    preact = jnp.dot(inputs, in_weight, preferred_element_type=jnp.float32) + in_bias
    hidden = jax.nn.silu(preact).astype(jnp.bfloat16)
    result = jnp.dot(hidden, out_weight, preferred_element_type=jnp.float32) + out_bias
    average = jnp.mean(result, axis=-1, keepdims=True)
    centred = result - average
    spread = jnp.mean(centred * centred, axis=-1, keepdims=True)
    return centred * lax.rsqrt(spread + 1e-05) * gain + shift


def body(
    fine_nodes,
    coarse_nodes,
    fine_edges,
    fine_senders,
    fine_receivers,
    fine_live,
    up_edges,
    up_senders,
    up_receivers,
    down_edges,
    down_senders,
    down_receivers,
    edge_in_weight,
    edge_in_bias,
    edge_out_weight,
    edge_out_bias,
    edge_gain,
    edge_shift,
    node_in_weight,
    node_in_bias,
    node_out_weight,
    node_out_bias,
    node_gain,
    node_shift,
):
    edge_params = (
        edge_in_weight,
        edge_in_bias,
        edge_out_weight,
        edge_out_bias,
        edge_gain,
        edge_shift,
    )
    node_params = (
        node_in_weight,
        node_in_bias,
        node_out_weight,
        node_out_bias,
        node_gain,
        node_shift,
    )
    node_count = fine_nodes.shape[0]
    fine_slots = fine_edges.shape[0]
    up_count = up_edges.shape[0]
    window = extended(fine_nodes, (("patch", 0),), RIM)
    gathered = lax.all_gather(coarse_nodes, ("group", "patch"), axis=0, tiled=True)
    coarse_count = gathered.shape[0]
    fine_in = jnp.concatenate(
        [fine_edges, window[fine_senders], fine_nodes[fine_receivers]], axis=1
    )
    up_in = jnp.concatenate([up_edges, fine_nodes[up_senders], gathered[up_receivers]], axis=1)
    down_in = jnp.concatenate(
        [down_edges, gathered[down_senders], fine_nodes[down_receivers]], axis=1
    )
    all_edges = jnp.concatenate([fine_edges, up_edges, down_edges], axis=0).astype(jnp.float32)
    updated = all_edges + perceptron(
        jnp.concatenate([fine_in, up_in, down_in], axis=0), *edge_params
    )
    live_mask = (jnp.arange(fine_slots) < fine_live[0])[:, None]
    fine_new = jnp.where(live_mask, updated[:fine_slots], all_edges[:fine_slots])
    up_new = updated[fine_slots : fine_slots + up_count]
    down_new = updated[fine_slots + up_count :]
    fine_sum = jax.ops.segment_sum(
        jnp.where(live_mask, fine_new, 0.0), fine_receivers, num_segments=node_count
    )
    fine_sum = (
        fine_sum + jax.ops.segment_sum(down_new, down_receivers, num_segments=node_count)
    ).astype(jnp.bfloat16)
    fine_out = fine_nodes.astype(jnp.float32) + perceptron(
        jnp.concatenate([fine_nodes, fine_sum], axis=1), *node_params
    )
    owned_count = coarse_nodes.shape[0]
    groups = lax.axis_size("group")
    patches = lax.axis_size("patch")
    partial_value = jax.ops.segment_sum(up_new, up_receivers, num_segments=coarse_count)
    partial_value = partial_value.reshape(groups, patches, owned_count, partial_value.shape[1])
    section_one = sent_and_summed(partial_value, "group", 0)
    coarse_total = sent_and_summed(section_one, "patch", 1).reshape(
        owned_count, partial_value.shape[3]
    )
    coarse_sum = coarse_total.astype(jnp.bfloat16)
    coarse_out = coarse_nodes.astype(jnp.float32) + perceptron(
        jnp.concatenate([coarse_nodes, coarse_sum], axis=1), *node_params
    )
    return (
        fine_out.astype(jnp.bfloat16),
        coarse_out.astype(jnp.bfloat16),
        fine_new.astype(jnp.bfloat16),
        up_new.astype(jnp.bfloat16),
        down_new.astype(jnp.bfloat16),
    )


def solution(mesh):
    return jax.shard_map(
        body,
        mesh=mesh,
        in_specs=(
            P(("group", "patch"), None),
            P(("group", "patch"), None),
            P(("group", "patch"), None),
            P(("group", "patch")),
            P(("group", "patch")),
            P(("group", "patch")),
            P(("group", "patch"), None),
            P(("group", "patch")),
            P(("group", "patch")),
            P(("group", "patch"), None),
            P(("group", "patch")),
            P(("group", "patch")),
            P(),
            P(),
            P(),
            P(),
            P(),
            P(),
            P(),
            P(),
            P(),
            P(),
            P(),
            P(),
        ),
        out_specs=(
            P(("group", "patch"), None),
            P(("group", "patch"), None),
            P(("group", "patch"), None),
            P(("group", "patch"), None),
            P(("group", "patch"), None),
        ),
        check_vma=False,
    )
```

profile of v0, /device:TPU:1, one launch (start us, length us, event | category | flops | bytes accessed | tf_op | source)
XLA Modules:
  0.0 490.3 jit_solution(15975151159262812078)
XLA Ops:
  12.0 5.3 %collective-permute-start.1 = (bf16[128,512]{1,0:T(8,128)(2,1)S(1)}, bf16[128,512]{1,0:T(8,128)(2,1)S(1)}, u32[]{:S(2)}, u32[]{:S(2)}) collective-permute-start(bf16[128,512]{1,0:T(8,128)(2,1)S(1)} %get-tuple-element.25), channel_id=1, source_target_pairs={{1,0},{2,1},{3,2},{4,3},{5,4},{6,5},{7,6},{8,7},{9,8},{10,9},{11,1... | collective-permute-start | bytes 393224 | tf_op jit(solution)/shard_map/ppermute | solution.py:17
  20.7 6.4 %copy.49 = bf16[4096,512]{0,1:T(8,128)(2,1)} copy(bf16[4096,512]{1,0:T(8,128)(2,1)} %param.26) | data formatting | bytes 8388608 | tf_op args[2]
  29.5 6.6 %maximum_convert_fusion = f32[5120,512]{0,1:T(8,128)} fusion(bf16[512,512]{0,1:T(8,128)(2,1)} %copy.51, bf16[512,512]{0,1:T(8,128)(2,1)S(1)} %copy.50, bf16[4096,512]{0,1:T(8,128)(2,1)} %copy.49), kind=kLoop, calls=%fused_computation.32 | loop fusion | flops 15728640 | bytes 15728640 | tf_op jit(solution)/shard_map/convert_element_type | solution.py:99
  44.2 18.5 %gather_fusion.1 = bf16[4096,512]{1,0:T(8,128)(2,1)} fusion(bf16[1024,512]{1,0:T(8,128)(2,1)S(1)} %copy-done.2, s32[4096]{0:T(1024)} %fusion.49), kind=kCustom, calls=%fused_computation.1 | custom fusion | bytes 8404992 | tf_op jit(solution)/shard_map/gather | solution.py:93
  64.6 18.9 %gather_fusion = bf16[4096,512]{1,0:T(8,128)(2,1)} fusion(bf16[1280,512]{1,0:T(8,128)(2,1)} %pad_maximum_fusion, s32[4096]{0:T(1024)S(1)} %fusion.48), kind=kCustom, calls=%fused_computation | custom fusion | bytes 8404992 | tf_op jit(solution)/shard_map/gather | solution.py:93
  83.5 232.3 %all-gather.2.cloned.1.call-done = bf16[2048,512]{1,0:T(8,128)(2,1)} async-done(((bf16[16,512]{1,0:T(8,128)(2,1)}), bf16[2048,512]{1,0:T(8,128)(2,1)}) %all-gather.2.cloned.1.call-update) | async-done | bytes 2097168 | tf_op jit(solution)/shard_map/all_gather | solution.py:90
  315.8 4.5 gather_fusion.3
  320.3 4.5 gather_fusion.4
  324.9 27.5 %multiply_convert_fusion.clone.1.clone.4 = bf16[5120,512]{1,0:T(8,128)(2,1)} fusion(bf16[1536,512]{1,0:T(8,128)(2,1)S(1)} %copy-done, bf16[512,512]{1,0:T(8,128)(2,1)} %gather_fusion.5, bf16[512,512]{1,0:T(8,128)(2,1)} %gather_fusion.4, bf16[512,512]{1,0:T(8,128)(2,1)} %param.33, bf16[512,512]{1,0:T(8,128)(2,1)} %gather_fusion.3, ...), kind=kOutput, calls=%fused_computation.29.clone.clone.clone.clone.clone.1 | convolution fusion | flops 8210350080 | bytes 22546432 | tf_op jit(solution)/shard_map/dot_general | solution.py:35
  352.4 5.3 %add_reduce_fusion = (f32[5120]{0:T(1024)S(1)}, f32[5120,512]{0,1:T(8,128)S(1)}) fusion(f32[512]{0:T(512)S(1)} %copy-done.17, bf16[512,512]{1,0:T(8,128)(2,1)S(1)} %copy-done.25, bf16[5120,512]{1,0:T(8,128)(2,1)} %multiply_convert_fusion.clone.1.clone.4), kind=kOutput, calls=%fused_computation.30 | convolution fusion | flops 2689592320 | bytes 16275456 | tf_op jit(solution)/shard_map/dot_general | solution.py:37
  360.0 3.1 add_add_fusion
  363.1 3.8 copy-done.3
  370.5 6.5 %scatter_custom_fusion.2 = f32[2048,512]{1,0:T(8,128)} fusion(s32[512]{0:T(512)} %param.32, f32[512,512]{1,0:T(8,128)} %copy.54, f32[]{:T(128)} %constant.9.clone.1), kind=kCustom, calls=%fused_computation.40 | custom fusion | flops 262144 | bytes 4194816 | tf_op jit(solution)/shard_map/scatter-add | solution.py:119
  377.0 5.2 %all-to-all-start = ((f32[4,1,32,16,512]{4,3,2,1,0:T(8,128)}), f32[4,1,32,16,512]{4,3,2,1,0:T(8,128)}, u32[]{:S(2)}, u32[]{:S(2)}) async-start(f32[4,1,32,16,512]{4,3,2,1,0:T(8,128)} %bitcast.17), calls=%async_computation | async-start | bytes 8388608 | tf_op jit(solution)/shard_map/all_to_all | solution.py:30
  382.2 9.5 %broadcast_select_fusion = f32[4096,512]{0,1:T(8,128)} fusion(pred[4096]{0:T(1024)(128)(4,1)S(1)} %copy-done.9, f32[5120,512]{0,1:T(8,128)} %maximum_convert_fusion, f32[5120,512]{0,1:T(8,128)} %copy-done.3), kind=kLoop, calls=%fused_computation.34 | loop fusion | flops 4194304 | bytes 25169920 | tf_op jit(solution)/shard_map/jit(_where)/select_n | solution.py:108
  393.1 5.7 %scatter_custom_fusion.1 = f32[1024,512]{1,0:T(8,128)} fusion(s32[512]{0:T(512)} %param.35, f32[512,512]{1,0:T(8,128)} %copy.53, f32[]{:T(128)} %constant.9.clone.1), kind=kCustom, calls=%fused_computation.53 | custom fusion | flops 262144 | bytes 2097664 | tf_op jit(solution)/shard_map/scatter-add | solution.py:111
  398.8 9.1 %copy.52 = f32[4096,512]{1,0:T(8,128)} copy(f32[4096,512]{0,1:T(8,128)} %broadcast_select_fusion) | data formatting | bytes 16777216 | tf_op jit(solution)/shard_map/jit(_where)/select_n | solution.py:108
  407.8 26.6 %scatter_custom_fusion = f32[1024,512]{1,0:T(8,128)} fusion(s32[4096]{0:T(1024)} %param.28, f32[4096,512]{1,0:T(8,128)} %copy.52, f32[]{:T(128)} %constant.9.clone.1), kind=kCustom, calls=%fused_computation.55 | custom fusion | flops 2097152 | bytes 2097664 | tf_op jit(solution)/shard_map/scatter-add | solution.py:107
  437.1 4.6 add_reduce_fusion.1
  441.7 8.3 %fusion.23 = bf16[4096,512]{0,1:T(8,128)(2,1)} fusion(f32[5120,512]{0,1:T(8,128)} %maximum_convert_fusion, f32[5120,512]{0,1:T(8,128)} %copy-done.3, pred[4096]{0:T(1024)(128)(4,1)S(1)} %copy-done.9), kind=kLoop, calls=%fused_computation.35 | loop fusion | flops 2097152 | bytes 12587008 | tf_op jit(solution)/shard_map/convert_element_type | solution.py:132
  450.0 3.7 reduce_sum.76
  453.8 7.9 %all-to-all-start.1 = ((f32[32,1,1,16,512]{4,3,2,1,0:T(8,128)}), f32[32,1,1,16,512]{4,3,2,1,0:T(8,128)}, u32[]{:S(2)}, u32[]{:S(2)}) async-start(f32[32,1,1,16,512]{4,3,2,1,0:T(8,128)} %bitcast.3), calls=%async_computation.1 | async-start | bytes 2097152 | tf_op jit(solution)/shard_map/all_to_all | solution.py:30
  465.4 6.5 %copy.57 = bf16[4096,512]{1,0:T(8,128)(2,1)} copy(bf16[4096,512]{0,1:T(8,128)(2,1)} %fusion.23) | data formatting | bytes 8388608
  473.9 3.3 add_convert_fusion
  (98 shorter events, 41.6 us)
Async XLA Ops:
  7.2 317.7 %copy-start = (bf16[1536,512]{1,0:T(8,128)(2,1)S(1)}, bf16[1536,512]{1,0:T(8,128)(2,1)}, u32[]{:S(2)}) copy-start(bf16[1536,512]{1,0:T(8,128)(2,1)} %param.36) | copy-start | bytes 4718596
  7.2 308.6 %all-gather.2.cloned.1.call-start = ((), (), s32[]{:S(2)}) async-start(), calls=%async_computation.2 | async-start | bytes 2113536 | tf_op jit(solution)/shard_map/all_gather | solution.py:90
  9.5 53.8 %collective-permute-start = (bf16[128,512]{1,0:T(8,128)(2,1)}, bf16[128,512]{1,0:T(8,128)(2,1)S(1)}, u32[]{:S(2)}, u32[]{:S(2)}) collective-permute-start(bf16[128,512]{1,0:T(8,128)(2,1)} %get-tuple-element.24), channel_id=1, source_target_pairs={{0,1},{1,2},{2,3},{3,4},{4,5},{5,6},{6,7},{7,8},{8,9},{9,10},{10,1... | collective-permute-start | bytes 393224 | tf_op jit(solution)/shard_map/ppermute | solution.py:16
  12.0 51.3 %collective-permute-start.1 = (bf16[128,512]{1,0:T(8,128)(2,1)S(1)}, bf16[128,512]{1,0:T(8,128)(2,1)S(1)}, u32[]{:S(2)}, u32[]{:S(2)}) collective-permute-start(bf16[128,512]{1,0:T(8,128)(2,1)S(1)} %get-tuple-element.25), channel_id=1, source_target_pairs={{1,0},{2,1},{3,2},{4,3},{5,4},{6,5},{7,6},{8,7},{9,8},{10,9},{11,1... | collective-permute-start | bytes 393224 | tf_op jit(solution)/shard_map/ppermute | solution.py:17
  20.6 7.0 %copy-start.20 = (s32[512]{0:T(512)S(1)}, s32[512]{0:T(512)}, u32[]{:S(2)}) copy-start(s32[512]{0:T(512)} %param.34) | copy-start | bytes 6148
  20.6 7.6 %copy-start.21 = (s32[512]{0:T(512)S(1)}, s32[512]{0:T(512)}, u32[]{:S(2)}) copy-start(s32[512]{0:T(512)} %param.32) | copy-start | bytes 6148
  20.6 8.2 %copy-start.22 = (s32[512]{0:T(512)S(1)}, s32[512]{0:T(512)}, u32[]{:S(2)}) copy-start(s32[512]{0:T(512)} %param.35) | copy-start | bytes 6148
  20.7 8.2 %copy-start.11 = (s32[4096]{0:T(1024)S(1)}, s32[4096]{0:T(1024)}, u32[]{:S(2)}) copy-start(s32[4096]{0:T(1024)} %param.27) | copy-start | bytes 49156
  20.7 8.2 %copy-start.12 = (s32[4096]{0:T(1024)S(1)}, s32[4096]{0:T(1024)}, u32[]{:S(2)}) copy-start(s32[4096]{0:T(1024)} %param.28) | copy-start | bytes 49156
  29.5 7.2 %copy-start.2 = (bf16[1024,512]{1,0:T(8,128)(2,1)S(1)}, bf16[1024,512]{1,0:T(8,128)(2,1)}, u32[]{:S(2)}) copy-start(bf16[1024,512]{1,0:T(8,128)(2,1)} %param.24) | copy-start | bytes 3145732
  64.6 251.2 %copy-start.14 = (s32[1024]{0:T(1024)S(1)}, s32[1024]{0:T(1024)}, u32[]{:S(2)}) copy-start(s32[1024]{0:T(1024)} %pad_clamp_fusion.2) | copy-start | bytes 12292
  83.4 236.9 %copy-start.13 = (s32[1024]{0:T(1024)S(1)}, s32[1024]{0:T(1024)}, u32[]{:S(2)}) copy-start(s32[1024]{0:T(1024)} %pad_clamp_fusion.1) | copy-start | bytes 12292
  83.5 241.4 %copy-start.26 = (f32[512]{0:T(512)S(1)}, f32[512]{0:T(512)}, u32[]{:S(2)}) copy-start(f32[512]{0:T(512)} %param.37) | copy-start | bytes 6148
  324.9 27.5 %copy-start.17 = (f32[512]{0:T(512)S(1)}, f32[512]{0:T(512)}, u32[]{:S(2)}) copy-start(f32[512]{0:T(512)} %param.39) | copy-start | bytes 6148
  324.9 27.5 %copy-start.25 = (bf16[512,512]{1,0:T(8,128)(2,1)S(1)}, bf16[512,512]{1,0:T(8,128)(2,1)}, u32[]{:S(2)}) copy-start(bf16[512,512]{1,0:T(8,128)(2,1)} %param.38) | copy-start | bytes 1572868
  377.0 73.0 %all-to-all-start = ((f32[4,1,32,16,512]{4,3,2,1,0:T(8,128)}), f32[4,1,32,16,512]{4,3,2,1,0:T(8,128)}, u32[]{:S(2)}, u32[]{:S(2)}) async-start(f32[4,1,32,16,512]{4,3,2,1,0:T(8,128)} %bitcast.17), calls=%async_computation | async-start | bytes 8388608 | tf_op jit(solution)/shard_map/all_to_all | solution.py:30
  407.8 29.2 %copy-start.7 = (bf16[512,512]{1,0:T(8,128)(2,1)S(1)}, bf16[512,512]{1,0:T(8,128)(2,1)}, u32[]{:S(2)}) copy-start(bf16[512,512]{1,0:T(8,128)(2,1)} %param.44) | copy-start | bytes 1572868
  407.8 29.2 %copy-start.10 = (f32[512]{0:T(512)S(1)}, f32[512]{0:T(512)}, u32[]{:S(2)}) copy-start(f32[512]{0:T(512)} %param.45) | copy-start | bytes 6148
  407.8 29.2 %copy-start.18 = (f32[512]{0:T(512)S(1)}, f32[512]{0:T(512)}, u32[]{:S(2)}) copy-start(f32[512]{0:T(512)} %param.43) | copy-start | bytes 6148
  453.8 25.7 %all-to-all-start.1 = ((f32[32,1,1,16,512]{4,3,2,1,0:T(8,128)}), f32[32,1,1,16,512]{4,3,2,1,0:T(8,128)}, u32[]{:S(2)}, u32[]{:S(2)}) async-start(f32[32,1,1,16,512]{4,3,2,1,0:T(8,128)} %bitcast.3), calls=%async_computation.1 | async-start | bytes 2097152 | tf_op jit(solution)/shard_map/all_to_all | solution.py:30
  465.4 8.5 %copy-start.6 = (bf16[1024,512]{0,1:T(8,128)(2,1)S(1)}, bf16[1024,512]{0,1:T(8,128)(2,1)}, u32[]{:S(2)}) copy-start(bf16[1024,512]{0,1:T(8,128)(2,1)} %copy.48) | copy-start | bytes 3145732
  465.4 8.5 %copy-start.15 = (f32[512]{0:T(512)S(1)}, f32[512]{0:T(512)}, u32[]{:S(2)}) copy-start(f32[512]{0:T(512)} %param.47) | copy-start | bytes 6148
  465.4 8.5 %copy-start.16 = (f32[512]{0:T(512)S(1)}, f32[512]{0:T(512)}, u32[]{:S(2)}) copy-start(f32[512]{0:T(512)} %param.46) | copy-start | bytes 6148
  473.8 9.6 %copy-start.1 = (bf16[1536,512]{1,0:T(8,128)(2,1)S(1)}, bf16[1536,512]{1,0:T(8,128)(2,1)}, u32[]{:S(2)}) copy-start(bf16[1536,512]{1,0:T(8,128)(2,1)} %param.36) | copy-start | bytes 4718596
  (8 other events, 31.4 us)
Sparse Core Ops, SparseCore 0:
  9.7 306.0 all-gather.1
where the time goes:
time: 492 us; the launch traced here: 490 us
  waiting for transfers between devices  233 us (47%)
  local copies, waits for them, and re-layouts  95.4 us (19%)
  other arithmetic  86.8 us (18%)
  matrix products  39.1 us (8%)
  starting transfers between devices  20.9 us (4%)
  between operations  15 us (3%)
    all_gather x1, waiting for transfers between devices, body(): lax.all_gather(coarse_nodes, ('group', 'patch'), axis=0, tiled=True)  232 us
    dot_general x1, matrix products, perceptron(): jnp.dot(inputs, in_weight, preferred_element_type=jnp.float32) + in_bias  27.5 us
    scatter-add x1, other arithmetic, body(): jax.ops.segment_sum(jnp.where(live_mask, fine_new, 0.0), fine_receivers,...  26.6 us
    unnamed x62, local copies, waits for them, and re-layouts  26 us
    gather x1, local copies, waits for them, and re-layouts, body(): window[fine_senders]  18.9 us
    gather x1, local copies, waits for them, and re-layouts, body(): fine_nodes[fine_receivers]  18.5 us
    all_to_all x2, starting transfers between devices, sent_and_summed(): parts = lax.all_to_all(split_up(shard, dim, size), axis, 0, 0, tiled=True)  13 us
    dot_general x3, matrix products, perceptron(): jnp.dot(hidden, out_weight, preferred_element_type=jnp.float32) + out_bias  11.7 us
  transfers between devices with their start and end apart: 5, of which 1 were waited for; matrix products, arithmetic and copies ran while one was open for 31% of the time, Pallas kernels for 0%

commit v1 on v0

v1 whole, which is shorter than its diff:
```python
import functools

import jax
import jax.numpy as jnp
from jax import lax
from jax.experimental import pallas as pl
from jax.experimental.pallas import tpu as pltpu
from jax.sharding import PartitionSpec as P

RIM = 128
BF = jnp.bfloat16
F32 = jnp.float32
TILE = 1024
BOTH = ("group", "patch")


def dot(a, b):
    return jnp.dot(a, b, preferred_element_type=F32)


def dot_t(a, b):
    return lax.dot_general(a, b, (((0,), (0,)), ((), ())), preferred_element_type=F32)


def one_hot_t(rows, index):
    iota = lax.broadcasted_iota(jnp.int32, (rows, 128), 0)
    blocks = [
        jnp.where(iota == index[j : j + 1, :], 1.0, 0.0).astype(BF) for j in range(index.shape[0])
    ]
    return jnp.concatenate(blocks, axis=1)


def silu(u):
    half = 0.5 * u
    return half + half * jnp.tanh(half)


def normed(r, gain, shift):
    centred = r - jnp.mean(r, axis=-1, keepdims=True)
    spread = jnp.mean(centred * centred, axis=-1, keepdims=True)
    return centred * lax.rsqrt(spread + 1e-05) * gain + shift


def tail(pre, out_weight, out_bias, gain, shift):
    hidden = silu(pre).astype(BF)
    return normed(dot(hidden, out_weight[...]) + out_bias[...], gain[...], shift[...])


def fine_kernel(
    live, senders, receivers, before, nodes, after, edges, w1, b1, w2, b2, gain, shift,
    new_edges, sums, by_sender, by_receiver,
):
    width = nodes.shape[1]
    count = nodes.shape[0]
    w_send = w1[width : 2 * width, :]
    by_sender[0:RIM, :] = dot(before[...], w_send).astype(BF)
    by_sender[RIM : RIM + count, :] = dot(nodes[...], w_send).astype(BF)
    by_sender[RIM + count : 2 * RIM + count, :] = dot(after[...], w_send).astype(BF)
    by_receiver[...] = dot(nodes[...], w1[2 * width : 3 * width, :]).astype(BF)
    sums[...] = jnp.zeros_like(sums)
    blocks = TILE // 128

    def step(t, carry):
        base = pl.multiple_of(t * TILE, TILE)
        rows = pl.multiple_of(t * blocks, blocks)
        edge = edges[pl.ds(base, TILE), :]
        from_sender = one_hot_t(count + 2 * RIM, senders[pl.ds(rows, blocks), :])
        from_receiver = one_hot_t(count, receivers[pl.ds(rows, blocks), :])
        pre = dot(edge, w1[0:width, :]) + b1[...]
        pre = pre + dot_t(from_sender, by_sender[...])
        pre = pre + dot_t(from_receiver, by_receiver[...])
        wide = edge.astype(F32)
        updated = wide + tail(pre, w2, b2, gain, shift)
        alive = lax.broadcasted_iota(jnp.int32, updated.shape, 0) + base < live[0]
        new_edges[pl.ds(base, TILE), :] = jnp.where(alive, updated, wide).astype(BF)
        sums[...] += dot(from_receiver, jnp.where(alive, updated, 0.0).astype(BF))
        return carry

    lax.fori_loop(0, edges.shape[0] // TILE, step, 0)


def cross_kernel(
    up_send, up_recv, down_send, down_recv, nodes, coarse, up, down, by_sender, by_receiver, sums,
    w1, b1, w2, b2, gain, shift, v1, c1, v2, c2, node_gain, node_shift,
    new_up, new_down, partial, fine_out,
):
    width = nodes.shape[1]
    count = nodes.shape[0]
    w_edge, w_send, w_recv = (w1[i * width : (i + 1) * width, :] for i in range(3))
    to_coarse = one_hot_t(coarse.shape[0], up_recv[...])
    pre = dot(up[...], w_edge) + b1[...]
    pre = pre + dot_t(one_hot_t(count, up_send[...]), by_sender[RIM : RIM + count, :])
    pre = pre + dot(dot_t(to_coarse, coarse[...]).astype(BF), w_recv)
    updated = (up[...].astype(F32) + tail(pre, w2, b2, gain, shift)).astype(BF)
    new_up[...] = updated
    partial[...] = dot(to_coarse, updated).astype(BF)

    to_fine = one_hot_t(count, down_recv[...])
    pre = dot(down[...], w_edge) + b1[...]
    pre = pre + dot(dot_t(one_hot_t(coarse.shape[0], down_send[...]), coarse[...]).astype(BF), w_send)
    pre = pre + dot_t(to_fine, by_receiver[...])
    updated = (down[...].astype(F32) + tail(pre, w2, b2, gain, shift)).astype(BF)
    new_down[...] = updated
    total = (sums[...] + dot(to_fine, updated)).astype(BF)

    pre = dot(nodes[...], v1[0:width, :]) + c1[...] + dot(total, v1[width : 2 * width, :])
    fine_out[...] = (nodes[...].astype(F32) + tail(pre, v2, c2, node_gain, node_shift)).astype(BF)


def coarse_kernel(parts, coarse, v1, c1, v2, c2, gain, shift, out):
    width = coarse.shape[1]
    total = jnp.sum(parts[...].astype(F32), axis=0).astype(BF)
    pre = dot(coarse[...], v1[0:width, :]) + c1[...] + dot(total, v1[width : 2 * width, :])
    out[...] = (coarse[...].astype(F32) + tail(pre, v2, c2, gain, shift)).astype(BF)


VM = pl.BlockSpec(memory_space=pltpu.VMEM)
SM = pl.BlockSpec(memory_space=pltpu.SMEM)


def call(kernel, outs, args, flops, smem=0):
    shapes = tuple(jax.ShapeDtypeStruct(s, d) for s, d in outs)
    moved = sum(a.size * a.dtype.itemsize for a in args)
    return pl.pallas_call(
        kernel,
        out_shape=shapes,
        in_specs=[SM] * smem + [VM] * (len(args) - smem),
        out_specs=tuple(VM for _ in shapes),
        compiler_params=pltpu.CompilerParams(vmem_limit_bytes=60 * 1024 * 1024),
        cost_estimate=pl.CostEstimate(flops=flops, bytes_accessed=moved, transcendentals=0),
    )(*args)


def swapped(parts, axis):
    return lax.all_to_all(parts, axis, 0, 0, tiled=True)


def body(
    fine_nodes, coarse_nodes, fine_edges, fine_senders, fine_receivers, fine_live,
    up_edges, up_senders, up_receivers, down_edges, down_senders, down_receivers,
    edge_in_weight, edge_in_bias, edge_out_weight, edge_out_bias, edge_gain, edge_shift,
    node_in_weight, node_in_bias, node_out_weight, node_out_bias, node_gain, node_shift,
):
    groups, patches = lax.axis_size("group"), lax.axis_size("patch")
    count, width = fine_nodes.shape
    owned = coarse_nodes.shape[0]
    slots = fine_edges.shape[0]
    lanes = lambda index: index.reshape(-1, 128)
    row = lambda vector: vector.reshape(1, -1)
    edge_net = (
        edge_in_weight, row(edge_in_bias), edge_out_weight, row(edge_out_bias), row(edge_gain),
        row(edge_shift),
    )
    node_net = (
        node_in_weight, row(node_in_bias), node_out_weight, row(node_out_bias), row(node_gain),
        row(node_shift),
    )
    ring = [(i, (i + 1) % patches) for i in range(patches)]
    before = lax.ppermute(fine_nodes[count - RIM :], "patch", ring)
    after = lax.ppermute(fine_nodes[:RIM], "patch", [(j, i) for i, j in ring])
    near = swapped(jnp.broadcast_to(coarse_nodes[None], (patches, owned, width)), "patch")
    near = near.reshape(1, patches * owned, width)
    coarse = swapped(jnp.broadcast_to(near, (groups, patches * owned, width)), "group")
    coarse = coarse.reshape(groups * patches * owned, width)

    new_edges, sums, by_sender, by_receiver = call(
        fine_kernel,
        (
            ((slots, width), BF), ((count, width), F32), ((count + 2 * RIM, width), BF),
            ((count, width), BF),
        ),
        (
            fine_live, lanes(fine_senders), lanes(fine_receivers), before, fine_nodes, after,
            fine_edges, *edge_net,
        ),
        30 * 10**9,
        smem=1,
    )
    new_up, new_down, partial, fine_out = call(
        cross_kernel,
        (
            (up_edges.shape, BF), (down_edges.shape, BF), (coarse.shape, BF), (fine_nodes.shape, BF),
        ),
        (
            lanes(up_senders), lanes(up_receivers), lanes(down_senders), lanes(down_receivers),
            fine_nodes, coarse, up_edges, down_edges, by_sender, by_receiver, sums,
            *edge_net, *node_net,
        ),
        8 * 10**9,
    )
    partial = swapped(partial.reshape(groups, patches, owned, width), "group")
    partial = jnp.sum(partial.astype(F32), axis=0).astype(BF)
    partial = swapped(partial, "patch")
    (coarse_out,) = call(
        coarse_kernel, ((coarse_nodes.shape, BF),), (partial, coarse_nodes, *node_net), 10**8
    )
    return fine_out, coarse_out, new_edges, new_up, new_down


def solution(mesh):
    rows, vector = P(BOTH, None), P(BOTH)
    return jax.shard_map(
        body,
        mesh=mesh,
        in_specs=(rows,) * 3 + (vector,) * 3 + (rows, vector, vector) * 2 + (P(),) * 12,
        out_specs=(rows,) * 5,
        check_vma=False,
    )
```

time: 492 us -> 127 us (0.26)
  waiting for transfers between devices: 233 us -> 2.94 us
  local copies, waits for them, and re-layouts: 95.4 us -> 6.04 us
  other arithmetic: 86.8 us -> 0.43 us
  Pallas kernels: 0 us -> 47.8 us
  blocking collectives: 0 us -> 44.6 us
  matrix products: 39.1 us -> 0 us
  between operations: 15 us -> 1.32 us
    all_gather x1 -> x0, waiting for transfers between devices: 232 us -> none  [body(): lax.all_gather(coarse_nodes, ('group', 'patch'), axis=0, tiled=True)]
    gather x6 -> x0, local copies, waits for them, and re-layouts: 52 us -> none  [the longest x1 18.9 us: body(): window[fine_senders]]
    pallas_call x0 -> x3, Pallas kernels: none -> 47.8 us  [call(): pl.pallas_call(kernel, out_shape=shapes, in_specs=[SM] * smem + [VM] * (l...]
    all_to_all x0 -> x2, blocking collectives: none -> 44.6 us  [swapped(): return lax.all_to_all(parts, axis, 0, 0, tiled=True)]
    dot_general x4 -> x0, matrix products: 39.1 us -> none  [the longest x1 27.5 us: perceptron(): jnp.dot(inputs, in_weight, preferred_element_type=jnp.float32) + in_bias]
    scatter-add x3 -> x0, other arithmetic: 38.8 us -> none  [the longest x1 26.6 us: body(): jax.ops.segment_sum(jnp.where(live_mask, fine_new, 0.0), fine_receivers,...]
    unnamed x62 -> x6, local copies, waits for them, and re-layouts: 26 us -> 2 us
    convert_element_type x5 -> x0, other arithmetic: 21.5 us -> none  [the longest x1 8.32 us: body(): fine_new.astype(jnp.bfloat16)]
  transfers between devices with their start and end apart: 5 -> 4, of which waited for: 1 -> 1; matrix products, arithmetic and copies ran while one was open for 31% -> 2% of each run, Pallas kernels for 0% -> 24%
where the time goes in v1:
time: 127 us; the launch traced here: 125 us
  Pallas kernels  47.8 us (38%)
  blocking collectives  44.6 us (35%)
  starting transfers between devices  22.2 us (17%)
  local copies, waits for them, and re-layouts  6.04 us (5%)
  waiting for transfers between devices  2.94 us (2%)
  between operations  1.32 us (1%)
    pallas_call x3, Pallas kernels, call(): pl.pallas_call(kernel, out_shape=shapes, in_specs=[SM] * smem + [VM] * (l...  47.8 us
    all_to_all x2, blocking collectives, swapped(): return lax.all_to_all(parts, axis, 0, 0, tiled=True)  44.6 us
    all_to_all x2, starting transfers between devices, swapped(): return lax.all_to_all(parts, axis, 0, 0, tiled=True)  16.6 us
    ppermute x1, starting transfers between devices, body(): after = lax.ppermute(fine_nodes[:RIM], 'patch', [(j, i) for i, j in ring])  5.61 us
    all_to_all x2, waiting for transfers between devices, swapped(): return lax.all_to_all(parts, axis, 0, 0, tiled=True)  2.94 us
  transfers between devices with their start and end apart: 4, of which 1 were waited for; matrix products, arithmetic and copies ran while one was open for 2% of the time, Pallas kernels for 24%

profile of v1, /device:TPU:1, one launch (start us, length us, event | category | flops | bytes accessed | tf_op | source)
XLA Modules:
  0.0 125.3 jit_solution(14354557500205087199)
XLA Ops:
  0.6 1.6 %broadcast_in_dim.6 = bf16[32,16,512]{2,1,0:T(8,128)(2,1)} broadcast(bf16[16,512]{1,0:T(8,128)(2,1)} %coarse.1), dimensions={1,2} | broadcast | bytes 540672 | tf_op jit(solution)/shard_map/broadcast_in_dim | solution.py:161
  2.2 9.7 %all-to-all-start = ((bf16[32,16,512]{2,1,0:T(8,128)(2,1)}), bf16[32,16,512]{2,1,0:T(8,128)(2,1)S(1)}, u32[]{:S(2)}, u32[]{:S(2)}) async-start(bf16[32,16,512]{2,1,0:T(8,128)(2,1)} %broadcast_in_dim.6), calls=%async_computation | async-start | bytes 1048576 | tf_op jit(solution)/shard_map/all_to_all | solution.py:135
  11.9 1.0 fusion
  12.9 5.6 %collective-permute-start.1 = (bf16[128,512]{1,0:T(8,128)(2,1)S(1)}, bf16[128,512]{1,0:T(8,128)(2,1)S(1)}, u32[]{:S(2)}, u32[]{:S(2)}) collective-permute-start(bf16[128,512]{1,0:T(8,128)(2,1)S(1)} %get-tuple-element.21), channel_id=1, source_target_pairs={{1,0},{2,1},{3,2},{4,3},{5,4},{6,5},{7,6},{8,7},{9,8},{10,9},{11,1... | collective-permute-start | bytes 393224 | tf_op jit(solution)/shard_map/ppermute | solution.py:160
  18.5 0.0 collective-permute-start
  19.2 2.9 %all-to-all-done = bf16[32,16,512]{2,1,0:T(8,128)(2,1)S(1)} async-done(((bf16[32,16,512]{2,1,0:T(8,128)(2,1)}), bf16[32,16,512]{2,1,0:T(8,128)(2,1)S(1)}, u32[]{:S(2)}, u32[]{:S(2)}) %all-to-all-start) | async-done | bytes 524320 | tf_op jit(solution)/shard_map/all_to_all | solution.py:135
  22.1 1.5 %broadcast_in_dim.15 = bf16[4,512,512]{2,1,0:T(8,128)(2,1)} broadcast(bf16[512,512]{1,0:T(8,128)(2,1)S(1)} %bitcast.17), dimensions={1,2} | broadcast | bytes 2621440 | tf_op jit(solution)/shard_map/broadcast_in_dim | solution.py:163
  23.6 6.9 %all-to-all-start.1 = ((bf16[4,512,512]{2,1,0:T(8,128)(2,1)}), bf16[4,512,512]{2,1,0:T(8,128)(2,1)S(1)}, u32[]{:S(2)}, u32[]{:S(2)}) async-start(bf16[4,512,512]{2,1,0:T(8,128)(2,1)} %broadcast_in_dim.15), calls=%async_computation.1 | async-start | bytes 4194304 | tf_op jit(solution)/shard_map/all_to_all | solution.py:135
  30.5 0.0 collective-permute-done.1.after
  30.5 0.0 copy-start.1
  30.5 0.0 collective-permute-done.before
  30.5 0.0 copy-start.2
  30.5 0.6 copy-done.1
  31.2 0.0 copy-done.2
  31.2 29.4 %shard_map.263 = (bf16[4096,512]{1,0:T(8,128)(2,1)}, f32[1024,512]{1,0:T(8,128)}, bf16[1280,512]{1,0:T(8,128)(2,1)}, bf16[1024,512]{1,0:T(8,128)(2,1)}) custom-call(s32[1]{0:T(128)S(6)} %copy.29.live, s32[32,128]{1,0:T(8,128)} %bitcast.28, s32[32,128]{1,0:T(8,128)} %bitcast.29, bf16[128,512]{1,0:T(8,128)(2,1)} %copy-done.2, bf16[1024,512]{1,0:T(8,128)(2,1)} %nodes.3, ...), custom_call_target="tpu_custom_call" | custom-call | flops 30000001024 | bytes 7643140 | tf_op jit(solution)/shard_map/pallas_call | solution.py:124
  60.6 0.0 all-to-all-done.1
  60.7 0.0 copy-start
  60.7 1.3 %copy-done = bf16[4,512,512]{2,1,0:T(8,128)(2,1)} copy-done((bf16[4,512,512]{2,1,0:T(8,128)(2,1)}, bf16[4,512,512]{2,1,0:T(8,128)(2,1)S(1)}, u32[]{:S(2)}) %copy-start) | copy-done | bytes 2097176
  62.0 15.5 %shard_map.264 = (bf16[512,512]{1,0:T(8,128)(2,1)}, bf16[512,512]{1,0:T(8,128)(2,1)}, bf16[2048,512]{1,0:T(8,128)(2,1)}, bf16[1024,512]{1,0:T(8,128)(2,1)}) custom-call(s32[4,128]{1,0:T(4,128)} %bitcast.30, s32[4,128]{1,0:T(4,128)} %bitcast.31, s32[4,128]{1,0:T(4,128)} %bitcast.32, s32[4,128]{1,0:T(4,128)} %bitcast.33, bf16[1024,512]{1,0:T(8,128)(2,1)} %nodes.3, ...), custom_call_target="tpu_custom_call" | custom-call | flops 8000000000 | bytes 12345344 | tf_op jit(solution)/shard_map/pallas_call | solution.py:124
  77.5 30.9 %all_to_all.20 = bf16[4,32,16,512]{3,2,1,0:T(8,128)(2,1)S(1)} all-to-all(bf16[4,32,16,512]{3,2,1,0:T(8,128)(2,1)} %bitcast.19), channel_id=1, replica_groups=mesh['group'=4,'patch'=32] {'group'}, dimensions={0} | all-to-all | bytes 4194304 | tf_op jit(solution)/shard_map/all_to_all | solution.py:135
  108.4 0.4 reduce_sum.12
  108.9 13.7 %all_to_all.21.parts = bf16[32,16,512]{2,1,0:T(8,128)(2,1)} all-to-all(bf16[32,16,512]{2,1,0:T(8,128)(2,1)S(1)} %reduce_sum.12), channel_id=1, replica_groups=mesh['group'=4,'patch'=32] {'patch'}, dimensions={0} | all-to-all | bytes 1048576 | tf_op jit(solution)/shard_map/all_to_all | solution.py:135
  122.5 2.8 %shard_map.265 = bf16[16,512]{1,0:T(8,128)(2,1)} custom-call(bf16[32,16,512]{2,1,0:T(8,128)(2,1)} %all_to_all.21.parts, bf16[16,512]{1,0:T(8,128)(2,1)} %coarse.1, bf16[1024,512]{1,0:T(8,128)(2,1)} %v1.3, f32[1,512]{1,0:T(1,128)} %bitcast.21, bf16[512,512]{1,0:T(8,128)(2,1)} %v2.3, f32[1,512]{1,0:T(1,128)} %bitcast.23, f32[1,512]{1,0:T(1,128)} %bitcast.25, ...), custom_call_target="tpu_custom_call" | custom-call | flops 100000000 | bytes 2121728 | tf_op jit(solution)/shard_map/pallas_call | solution.py:124
Async XLA Ops:
  2.2 19.9 %all-to-all-start = ((bf16[32,16,512]{2,1,0:T(8,128)(2,1)}), bf16[32,16,512]{2,1,0:T(8,128)(2,1)S(1)}, u32[]{:S(2)}, u32[]{:S(2)}) async-start(bf16[32,16,512]{2,1,0:T(8,128)(2,1)} %broadcast_in_dim.6), calls=%async_computation | async-start | bytes 1048576 | tf_op jit(solution)/shard_map/all_to_all | solution.py:135
  12.9 17.6 %collective-permute-start.1 = (bf16[128,512]{1,0:T(8,128)(2,1)S(1)}, bf16[128,512]{1,0:T(8,128)(2,1)S(1)}, u32[]{:S(2)}, u32[]{:S(2)}) collective-permute-start(bf16[128,512]{1,0:T(8,128)(2,1)S(1)} %get-tuple-element.21), channel_id=1, source_target_pairs={{1,0},{2,1},{3,2},{4,3},{5,4},{6,5},{7,6},{8,7},{9,8},{10,9},{11,1... | collective-permute-start | bytes 393224 | tf_op jit(solution)/shard_map/ppermute | solution.py:160
  18.5 12.0 %collective-permute-start = (bf16[128,512]{1,0:T(8,128)(2,1)S(1)}, bf16[128,512]{1,0:T(8,128)(2,1)S(1)}, u32[]{:S(2)}, u32[]{:S(2)}) collective-permute-start(bf16[128,512]{1,0:T(8,128)(2,1)S(1)} %get-tuple-element.22), channel_id=1, source_target_pairs={{0,1},{1,2},{2,3},{3,4},{4,5},{5,6},{6,7},{7,8},{8,9},{9,10},{10,1... | collective-permute-start | bytes 393224 | tf_op jit(solution)/shard_map/ppermute | solution.py:159
  23.6 37.1 %all-to-all-start.1 = ((bf16[4,512,512]{2,1,0:T(8,128)(2,1)}), bf16[4,512,512]{2,1,0:T(8,128)(2,1)S(1)}, u32[]{:S(2)}, u32[]{:S(2)}) async-start(bf16[4,512,512]{2,1,0:T(8,128)(2,1)} %broadcast_in_dim.15), calls=%async_computation.1 | async-start | bytes 4194304 | tf_op jit(solution)/shard_map/all_to_all | solution.py:135
  30.5 0.7 copy-start.1
  30.5 0.7 copy-start.2
  60.7 1.3 %copy-start = (bf16[4,512,512]{2,1,0:T(8,128)(2,1)}, bf16[4,512,512]{2,1,0:T(8,128)(2,1)S(1)}, u32[]{:S(2)}) copy-start(bf16[4,512,512]{2,1,0:T(8,128)(2,1)S(1)} %all-to-all-done.1) | copy-start | bytes 6291460

commit v2 on v1

v2 whole, which is shorter than its diff:
```python
import functools

import jax
import jax.numpy as jnp
from jax import lax
from jax.experimental import pallas as pl
from jax.experimental.pallas import tpu as pltpu
from jax.sharding import PartitionSpec as P

RIM = 128
BF = jnp.bfloat16
F32 = jnp.float32
TILE = 1024
BOTH = ("group", "patch")
MESH = pl.DeviceIdType.MESH


def dot(a, b):
    return jnp.dot(a, b, preferred_element_type=F32)


def dot_t(a, b):
    return lax.dot_general(a, b, (((0,), (0,)), ((), ())), preferred_element_type=F32)


def one_hot_t(rows, index):
    iota = lax.broadcasted_iota(jnp.int32, (rows, 128), 0)
    blocks = [
        jnp.where(iota == index[j : j + 1, :], 1.0, 0.0).astype(BF) for j in range(index.shape[0])
    ]
    return jnp.concatenate(blocks, axis=1)


def silu(u):
    half = 0.5 * u
    return half + half * jnp.tanh(half)


def normed(r, gain, shift):
    centred = r - jnp.mean(r, axis=-1, keepdims=True)
    spread = jnp.mean(centred * centred, axis=-1, keepdims=True)
    return centred * lax.rsqrt(spread + 1e-05) * gain + shift


def tail(pre, out_weight, out_bias, gain, shift):
    hidden = silu(pre).astype(BF)
    return normed(dot(hidden, out_weight[...]) + out_bias[...], gain[...], shift[...])


def kernel(
    groups, patches,
    live, senders, receivers, up_send, up_recv, down_send, down_recv,
    b1, b2, gain, shift, c1, c2, node_gain, node_shift,
    nodes, coarse, edges, up, down, w1_in, w2_in, v1_in, v2_in,
    fine_out, coarse_out, edges_out, up_out, down_out,
    win, eb, ub, db, w1, w2, v1, v2, by_sender, by_receiver, pre, sums, table, part, beside, half,
    landed, fine_new, coarse_new, up_pre, down_pre,
    load, store, rim_sent, rim_got, spread_sent, spread_got, twin_sent, twin_got, home_sent, home_got,
):
    count, width = nodes.shape
    slots = edges.shape[0]
    owned = coarse.shape[0]
    g, p = lax.axis_index("group"), lax.axis_index("patch")
    core, high = lax.rem(g, 2), g // 2
    chips = groups // 2 * patches
    side = chips * owned
    me = high * patches + p
    twin = (high * 2 + 1 - core, p)
    mine = pl.ds(pl.multiple_of(me * owned, owned), owned)

    def partner(k):
        other = lax.rem(me + k, chips)
        return other, (other // patches * 2 + core, lax.rem(other, patches))

    def each_partner(action):
        def one(k, carry):
            action(*partner(k))
            return carry

        lax.fori_loop(1, chips, one, 0)

    def remote(source, target, sent, got, device):
        return pltpu.make_async_remote_copy(
            source, target, sent, got, device_id=device, device_id_type=MESH
        )

    def settle(ref, sem):
        pltpu.make_async_copy(ref, ref, sem).wait()

    barrier = pltpu.get_barrier_semaphore()

    def greet(other, device):
        pl.semaphore_signal(barrier, inc=1, device_id=device, device_id_type=MESH)

    greet(0, twin)
    each_partner(greet)

    body = pl.ds(RIM, count)
    steps = slots // TILE
    tile = lambda t: pl.ds(pl.multiple_of(t * TILE, TILE), TILE)
    get_nodes = pltpu.make_async_copy(nodes, win.at[body], load.at[0])
    get_w1 = pltpu.make_async_copy(w1_in, w1, load.at[1])
    get_own = pltpu.make_async_copy(coarse, table.at[mine], load.at[2])
    get_w2 = pltpu.make_async_copy(w2_in, w2, load.at[3])
    get_up = pltpu.make_async_copy(up, ub, load.at[4])
    get_down = pltpu.make_async_copy(down, db, load.at[5])
    get_v1 = pltpu.make_async_copy(v1_in, v1, load.at[6])
    get_v2 = pltpu.make_async_copy(v2_in, v2, load.at[7])
    get_edges = lambda t: pltpu.make_async_copy(edges.at[tile(t)], eb.at[tile(t)], load.at[8 + t])
    put_up = pltpu.make_async_copy(ub, up_out, store.at[0])
    put_down = pltpu.make_async_copy(db, down_out, store.at[1])
    put_fine = pltpu.make_async_copy(fine_new, fine_out, store.at[2])
    put_coarse = pltpu.make_async_copy(coarse_new, coarse_out, store.at[3])
    put_edges = lambda t: pltpu.make_async_copy(
        eb.at[tile(t)], edges_out.at[tile(t)], store.at[4 + t]
    )
    get_nodes.start()
    get_w1.start()
    get_own.start()
    get_edges(0).start()
    get_w2.start()
    get_up.start()
    get_down.start()
    for t in range(1, steps):
        get_edges(t).start()
    get_v1.start()
    get_v2.start()

    before = (g, lax.rem(p + patches - 1, patches))
    after = (g, lax.rem(p + 1, patches))
    to_after = remote(
        nodes.at[pl.ds(count - RIM, RIM)], win.at[pl.ds(0, RIM)], rim_sent.at[0], rim_got.at[0], after
    )
    to_before = remote(
        nodes.at[pl.ds(0, RIM)], win.at[pl.ds(RIM + count, RIM)], rim_sent.at[1], rim_got.at[1], before
    )
    same = pl.ds(0, side)
    other_side = pl.ds(side, side)
    table_over = remote(
        table.at[same], table.at[other_side], twin_sent.at[0], twin_got.at[0], twin
    )
    part_over = remote(part.at[other_side], beside, twin_sent.at[1], twin_got.at[1], twin)
    all_but_one = pl.ds(0, side - owned)

    def local_row(index):
        owner, inner = index // (patches * owned), lax.rem(index, patches * owned)
        away = jnp.where(lax.rem(owner, 2) == core, 0, side)
        return owner // 2 * (patches * owned) + inner + away

    get_nodes.wait()
    get_w1.wait()
    w_edge, w_send, w_recv = (w1.at[pl.ds(i * width, width)] for i in range(3))
    by_sender[RIM : RIM + count, :] = dot(win[RIM : RIM + count, :], w_send[...]).astype(BF)
    by_receiver[...] = dot(win[RIM : RIM + count, :], w_recv[...]).astype(BF)
    sums[...] = jnp.zeros_like(sums)

    pl.semaphore_wait(barrier, chips)
    to_after.start()
    to_before.start()

    def spread(other, device):
        remote(coarse, table.at[mine], spread_sent, spread_got, device).start()

    each_partner(spread)
    blocks = TILE // 128

    def up_stage():
        settle(table.at[all_but_one], spread_got)
        get_own.wait()
        table_over.start()
        get_up.wait()
        get_down.wait()
        up_pre[...] = (
            dot(ub[...], w_edge[...])
            + b1[...]
            + dot_t(one_hot_t(count, up_send[...]), by_sender[RIM : RIM + count, :])
        )
        down_pre[...] = (
            dot(db[...], w_edge[...])
            + b1[...]
            + dot_t(one_hot_t(count, down_recv[...]), by_receiver[...])
        )
        table_over.wait_recv()
        to_coarse = one_hot_t(2 * side, local_row(up_recv[...]))
        picked = dot_t(to_coarse, table[...]).astype(BF)
        new = tail(up_pre[...] + dot(picked, w_recv[...]), w2, b2, gain, shift)
        new = (ub[...].astype(F32) + new).astype(BF)
        ub[...] = new
        put_up.start()
        part[...] = dot(to_coarse, new).astype(BF)
        part_over.start()

    def home_stage():
        part_over.wait_recv()
        half[...] = (part[0:side, :].astype(F32) + beside[...].astype(F32)).astype(BF)
        landed[mine, :] = half[mine, :]

        def home(other, device):
            rows = pl.ds(pl.multiple_of(other * owned, owned), owned)
            remote(half.at[rows], landed.at[mine], home_sent, home_got, device).start()

        each_partner(home)

    def step(t, carry):
        base = pl.multiple_of(t * TILE, TILE)
        rows = pl.ds(pl.multiple_of(t * blocks, blocks), blocks)
        pl.when(t == steps // 2)(up_stage)
        pl.when(t == steps // 2 + 1)(home_stage)
        get_edges(t).wait()
        send_row = senders[rows, :]
        from_receiver = one_hot_t(count, receivers[rows, :])
        pre[...] = (
            dot(eb[tile(t), :], w_edge[...])
            + b1[...]
            + dot_t(one_hot_t(count, send_row - RIM), by_sender[RIM : RIM + count, :])
            + dot_t(from_receiver, by_receiver[...])
        )

        @pl.when(t == 0)
        def _():
            to_after.wait_recv()
            to_before.wait_recv()
            by_sender[0:RIM, :] = dot(win[0:RIM, :], w_send[...]).astype(BF)
            by_sender[RIM + count :, :] = dot(win[RIM + count :, :], w_send[...]).astype(BF)

        full = (
            pre[...]
            + dot_t(one_hot_t(RIM, send_row), by_sender[0:RIM, :])
            + dot_t(one_hot_t(RIM, send_row - (RIM + count)), by_sender[RIM + count :, :])
        )
        wide = eb[tile(t), :].astype(F32)
        updated = wide + tail(full, w2, b2, gain, shift)
        alive = lax.broadcasted_iota(jnp.int32, updated.shape, 0) + base < live[0]
        sums[...] += dot(
            one_hot_t(count, receivers[rows, :]), jnp.where(alive, updated, 0.0).astype(BF)
        )
        eb[tile(t), :] = jnp.where(alive, updated, wide).astype(BF)
        put_edges(t).start()
        return carry

    get_w2.wait()
    lax.fori_loop(0, steps, step, 0)

    picked = dot_t(one_hot_t(2 * side, local_row(down_send[...])), table[...]).astype(BF)
    new = tail(down_pre[...] + dot(picked, w_send[...]), w2, b2, gain, shift)
    new = (db[...].astype(F32) + new).astype(BF)
    db[...] = new
    put_down.start()
    total = (sums[...] + dot(one_hot_t(count, down_recv[...]), new)).astype(BF)
    get_v1.wait()
    get_v2.wait()

    def node_net(old, summed):
        inner = dot(old, v1[0:width, :]) + c1[...] + dot(summed, v1[width : 2 * width, :])
        return (old.astype(F32) + tail(inner, v2, c2, node_gain, node_shift)).astype(BF)

    fine_new[...] = node_net(win[RIM : RIM + count, :], total)
    put_fine.start()

    settle(landed.at[all_but_one], home_got)
    arrived = jnp.sum(landed[...].astype(F32).reshape(chips, owned, width), axis=0).astype(BF)
    coarse_new[...] = node_net(table[mine, :], arrived)
    put_coarse.start()

    to_after.wait_send()
    to_before.wait_send()
    settle(table.at[all_but_one], spread_sent)
    settle(half.at[all_but_one], home_sent)
    table_over.wait_send()
    part_over.wait_send()
    for copy in (put_up, put_down, put_fine, put_coarse):
        copy.wait()
    for t in range(steps):
        put_edges(t).wait()


def body(
    fine_nodes, coarse_nodes, fine_edges, fine_senders, fine_receivers, fine_live,
    up_edges, up_senders, up_receivers, down_edges, down_senders, down_receivers,
    edge_in_weight, edge_in_bias, edge_out_weight, edge_out_bias, edge_gain, edge_shift,
    node_in_weight, node_in_bias, node_out_weight, node_out_bias, node_gain, node_shift,
):
    groups, patches = lax.axis_size("group"), lax.axis_size("patch")
    count, width = fine_nodes.shape
    owned = coarse_nodes.shape[0]
    slots = fine_edges.shape[0]
    crossing = up_edges.shape[0]
    everywhere = groups * patches * owned
    side = everywhere // 2
    steps = slots // TILE
    lanes = lambda index: index.reshape(-1, 128)
    row = lambda vector: vector.reshape(1, -1)
    vm = pl.BlockSpec(memory_space=pltpu.VMEM)
    anywhere = pl.BlockSpec(memory_space=pl.ANY)
    outs = (fine_nodes, coarse_nodes, fine_edges, up_edges, down_edges)
    rows = lambda n, dtype=BF: pltpu.VMEM((n, width), dtype)
    dma = pltpu.SemaphoreType.DMA
    return pl.pallas_call(
        functools.partial(kernel, groups, patches),
        out_shape=tuple(jax.ShapeDtypeStruct(a.shape, a.dtype) for a in outs),
        in_specs=[pl.BlockSpec(memory_space=pltpu.SMEM)] + [vm] * 14 + [anywhere] * 9,
        out_specs=(anywhere,) * 5,
        scratch_shapes=[
            rows(count + 2 * RIM), rows(slots), rows(crossing), rows(crossing),
            rows(3 * width), rows(width), rows(2 * width), rows(width),
            rows(count + 2 * RIM), rows(count), rows(TILE, F32), rows(count, F32),
            rows(everywhere), rows(everywhere), rows(side), rows(side), rows(side),
            rows(count), rows(owned), rows(crossing, F32), rows(crossing, F32),
            dma((8 + steps,)), dma((4 + steps,)), dma((2,)), dma((2,)),
            dma(()), dma(()), dma((2,)), dma((2,)), dma(()), dma(()),
        ],
        compiler_params=pltpu.CompilerParams(
            vmem_limit_bytes=62 * 1024 * 1024, collective_id=0, has_side_effects=True
        ),
    )(
        fine_live, lanes(fine_senders), lanes(fine_receivers), lanes(up_senders),
        lanes(up_receivers), lanes(down_senders), lanes(down_receivers),
        row(edge_in_bias), row(edge_out_bias), row(edge_gain), row(edge_shift),
        row(node_in_bias), row(node_out_bias), row(node_gain), row(node_shift),
        fine_nodes, coarse_nodes, fine_edges, up_edges, down_edges,
        edge_in_weight, edge_out_weight, node_in_weight, node_out_weight,
    )


def solution(mesh):
    rows, vector = P(BOTH, None), P(BOTH)
    return jax.shard_map(
        body,
        mesh=mesh,
        in_specs=(rows,) * 3 + (vector,) * 3 + (rows, vector, vector) * 2 + (P(),) * 12,
        out_specs=(rows,) * 5,
        check_vma=False,
    )
```

time: 127 us -> 76.2 us (0.60); the launches traced: 125 us -> 75.9 us
  blocking collectives: 44.6 us -> 0 us
  starting transfers between devices: 22.2 us -> 0 us
  Pallas kernels: 47.8 us -> 64.9 us
  local copies, waits for them, and re-layouts: 6.04 us -> 9.74 us
  waiting for transfers between devices: 2.94 us -> 0 us
    all_to_all x2 -> x0, blocking collectives: 44.6 us -> none  [swapped(): return lax.all_to_all(parts, axis, 0, 0, tiled=True)]
    pallas_call x3 -> x1, Pallas kernels: 47.8 us -> 64.9 us  [body(): pl.pallas_call(functools.partial(kernel, groups, patches), out_shape=tupl...]
    all_to_all x2 -> x0, starting transfers between devices: 16.6 us -> none  [swapped(): return lax.all_to_all(parts, axis, 0, 0, tiled=True)]
    unnamed x6 -> x9, local copies, waits for them, and re-layouts: 2 us -> 9.74 us
    ppermute x2 -> x0, starting transfers between devices: 5.61 us -> none  [the longest x1 5.61 us: body(): after = lax.ppermute(fine_nodes[:RIM], 'patch', [(j, i) for i, j in ring])]
    broadcast_in_dim x2 -> x0, local copies, waits for them, and re-layouts: 3.05 us -> none  [the longest x1 1.57 us: body(): jnp.broadcast_to(coarse_nodes[None], (patches, owned, width))]
    all_to_all x2 -> x0, waiting for transfers between devices: 2.94 us -> none  [swapped(): return lax.all_to_all(parts, axis, 0, 0, tiled=True)]
  transfers between devices with their start and end apart: 4 -> 0, of which waited for: 1 -> 0; matrix products, arithmetic and copies ran while one was open for 2% -> 0% of each run, Pallas kernels for 24% -> 0%
where the time goes in v2:
time: 76.2 us; the launch traced here: 75.9 us
  Pallas kernels  64.9 us (85%)
  local copies, waits for them, and re-layouts  9.74 us (13%)
  between operations  1.3 us (2%)
    pallas_call x1, Pallas kernels, body(): pl.pallas_call(functools.partial(kernel, groups, patches), out_shape=tupl...  64.9 us
    unnamed x9, local copies, waits for them, and re-layouts  9.74 us

profile of v2, /device:TPU:1, one launch (start us, length us, event | category | flops | bytes accessed | tf_op | source)
XLA Modules:
  0.0 75.9 jit_solution(15918680535979393430)
XLA Ops:
  1.3 64.9 %shard_map.263 = (bf16[1024,512]{1,0:T(8,128)(2,1)}, bf16[16,512]{1,0:T(8,128)(2,1)}, bf16[4096,512]{1,0:T(8,128)(2,1)}, bf16[512,512]{1,0:T(8,128)(2,1)}, bf16[512,512]{1,0:T(8,128)(2,1)}) custom-call(s32[1]{0:T(128)S(6)} %copy.34.live, s32[32,128]{1,0:T(8,128)} %bitcast.14, s32[32,128]{1,0:T(8,128)} %bitcast.15, s32[4,128]{1,0:T(4,128)} %bitcast.16, ...), custom_call_target="tpu_custom_call" | custom-call | tf_op jit(solution)/shard_map/pallas_call | solution.py:298
  66.2 2.3 %copy.35 = bf16[1024,512]{1,0:T(8,128)(2,1)} copy(bf16[1024,512]{1,0:T(8,128)(2,1)} %get-tuple-element.10) | data formatting | bytes 2097152
  68.4 1.3 %copy.36 = bf16[16,512]{1,0:T(8,128)(2,1)} copy(bf16[16,512]{1,0:T(8,128)(2,1)} %get-tuple-element.11) | data formatting | bytes 32768
  69.8 0.0 copy-start.1
  69.8 0.0 copy-start
  69.8 4.6 %copy.37 = bf16[4096,512]{1,0:T(8,128)(2,1)} copy(bf16[4096,512]{1,0:T(8,128)(2,1)} %get-tuple-element.12) | data formatting | bytes 8388608
  74.3 0.0 copy-done.1
  74.3 0.8 %copy.38 = bf16[512,512]{1,0:T(8,128)(2,1)} copy(bf16[512,512]{1,0:T(8,128)(2,1)S(1)} %copy-done.1) | data formatting | bytes 1048576
  75.1 0.0 copy-done
  75.1 0.8 %copy.39 = bf16[512,512]{1,0:T(8,128)(2,1)} copy(bf16[512,512]{1,0:T(8,128)(2,1)S(1)} %copy-done) | data formatting | bytes 1048576
Async XLA Ops:
  69.8 4.6 %copy-start.1 = (bf16[512,512]{1,0:T(8,128)(2,1)S(1)}, bf16[512,512]{1,0:T(8,128)(2,1)}, u32[]{:S(2)}) copy-start(bf16[512,512]{1,0:T(8,128)(2,1)} %get-tuple-element.13) | copy-start | bytes 1572868
  69.8 5.4 %copy-start = (bf16[512,512]{1,0:T(8,128)(2,1)S(1)}, bf16[512,512]{1,0:T(8,128)(2,1)}, u32[]{:S(2)}) copy-start(bf16[512,512]{1,0:T(8,128)(2,1)} %get-tuple-element.14) | copy-start | bytes 1572868

commit v3 on v2

v3 whole, which is shorter than its diff:
```python
import functools

import jax
import jax.numpy as jnp
from jax import lax
from jax.experimental import pallas as pl
from jax.experimental.pallas import tpu as pltpu
from jax.sharding import PartitionSpec as P

RIM = 128
BF = jnp.bfloat16
F32 = jnp.float32
TILE = 1024
BOTH = ("group", "patch")
MESH = pl.DeviceIdType.MESH


def dot(a, b):
    return jnp.dot(a, b, preferred_element_type=F32)


def dot_t(a, b):
    return lax.dot_general(a, b, (((0,), (0,)), ((), ())), preferred_element_type=F32)


def one_hot_t(rows, index):
    iota = lax.broadcasted_iota(jnp.int32, (rows, 128), 0)
    blocks = [
        jnp.where(iota == index[j : j + 1, :], 1.0, 0.0).astype(BF) for j in range(index.shape[0])
    ]
    return jnp.concatenate(blocks, axis=1)


def silu(u):
    half = 0.5 * u
    return half + half * jnp.tanh(half)


def normed(r, gain, shift):
    centred = r - jnp.mean(r, axis=-1, keepdims=True)
    spread = jnp.mean(centred * centred, axis=-1, keepdims=True)
    return centred * lax.rsqrt(spread + 1e-05) * gain + shift


def tail(pre, out_weight, out_bias, gain, shift):
    hidden = silu(pre).astype(BF)
    return normed(dot(hidden, out_weight[...]) + out_bias[...], gain[...], shift[...])


def kernel(
    groups, patches,
    live, senders_in, receivers_in, up_send_in, up_recv_in, down_send_in, down_recv_in,
    b1_in, b2_in, gain_in, shift_in, c1_in, c2_in, node_gain_in, node_shift_in,
    nodes, coarse, edges, up, down, w1_in, w2_in, v1_in, v2_in,
    fine_new, coarse_new, eb, ub, db,
    win, w1, w2, v1, v2, by_sender, by_receiver, pre, sums, table, part, beside, half,
    landed, up_pre, down_pre,
    senders, receivers, up_send, up_recv, down_send, down_recv,
    b1, b2, gain, shift, c1, c2, node_gain, node_shift,
    load, few, rim_sent, rim_got, spread_sent, spread_got, twin_sent, twin_got, home_sent, home_got,
):
    count, width = nodes.shape
    slots = edges.shape[0]
    owned = coarse.shape[0]
    g, p = lax.axis_index("group"), lax.axis_index("patch")
    core, high = lax.rem(g, 2), g // 2
    chips = groups // 2 * patches
    side = chips * owned
    me = high * patches + p
    twin = (high * 2 + 1 - core, p)
    mine = pl.ds(pl.multiple_of(me * owned, owned), owned)

    def each_partner(action):
        def one(k, carry):
            other = lax.rem(me + k, chips)
            action(other, (other // patches * 2 + core, lax.rem(other, patches)))
            return carry

        lax.fori_loop(1, chips, one, 0)

    def remote(source, target, sent, got, device):
        return pltpu.make_async_remote_copy(
            source, target, sent, got, device_id=device, device_id_type=MESH
        )

    def settle(ref, sem):
        pltpu.make_async_copy(ref, ref, sem).wait()

    barrier = pltpu.get_barrier_semaphore()

    def greet(other, device):
        pl.semaphore_signal(barrier, inc=1, device_id=device, device_id_type=MESH)

    greet(0, twin)
    each_partner(greet)

    steps = slots // TILE
    early = steps - 1
    tile = lambda t: pl.ds(pl.multiple_of(t * TILE, TILE), TILE)
    own_rows = slice(RIM, RIM + count)
    get_nodes = pltpu.make_async_copy(nodes, win.at[pl.ds(RIM, count)], load.at[0])
    get_w1 = pltpu.make_async_copy(w1_in, w1, load.at[1])
    get_own = pltpu.make_async_copy(coarse, table.at[mine], load.at[2])
    get_w2 = pltpu.make_async_copy(w2_in, w2, load.at[3])
    get_up = pltpu.make_async_copy(up, ub, load.at[4])
    get_down = pltpu.make_async_copy(down, db, load.at[5])
    get_v1 = pltpu.make_async_copy(v1_in, v1, load.at[6])
    get_v2 = pltpu.make_async_copy(v2_in, v2, load.at[7])
    get_edges = lambda t: pltpu.make_async_copy(edges.at[tile(t)], eb.at[tile(t)], load.at[8 + t])
    small = (
        (senders_in, senders), (receivers_in, receivers), (up_send_in, up_send),
        (up_recv_in, up_recv), (down_send_in, down_send), (down_recv_in, down_recv),
        (b1_in, b1), (b2_in, b2), (gain_in, gain), (shift_in, shift), (c1_in, c1), (c2_in, c2),
        (node_gain_in, node_gain), (node_shift_in, node_shift),
    )
    small = [pltpu.make_async_copy(a, b, few.at[i]) for i, (a, b) in enumerate(small)]
    get_nodes.start()
    get_w1.start()
    for copy in small:
        copy.start()
    get_own.start()
    get_up.start()
    get_down.start()
    for t in range(early):
        get_edges(t).start()
    get_w2.start()
    get_edges(early).start()
    get_v1.start()
    get_v2.start()

    before = (g, lax.rem(p + patches - 1, patches))
    after = (g, lax.rem(p + 1, patches))
    to_after = remote(
        nodes.at[pl.ds(count - RIM, RIM)], win.at[pl.ds(0, RIM)], rim_sent.at[0], rim_got.at[0], after
    )
    to_before = remote(
        nodes.at[pl.ds(0, RIM)], win.at[pl.ds(RIM + count, RIM)], rim_sent.at[1], rim_got.at[1], before
    )
    same = pl.ds(0, side)
    other_side = pl.ds(side, side)
    table_over = remote(
        table.at[same], table.at[other_side], twin_sent.at[0], twin_got.at[0], twin
    )
    part_over = remote(part.at[other_side], beside, twin_sent.at[1], twin_got.at[1], twin)
    all_but_one = pl.ds(0, side - owned)

    def spread(other, device):
        remote(coarse, table.at[mine], spread_sent, spread_got, device).start()

    with jax.named_scope("wait_bar"):
        pl.semaphore_wait(barrier, chips)
    each_partner(spread)
    to_after.start()
    to_before.start()

    def local_row(index):
        owner, inner = index // (patches * owned), lax.rem(index, patches * owned)
        away = jnp.where(lax.rem(owner, 2) == core, 0, side)
        return owner // 2 * (patches * owned) + inner + away

    with jax.named_scope("wait_load"):
        get_nodes.wait()
        get_w1.wait()
    w_edge, w_send, w_recv = (w1.at[pl.ds(i * width, width)] for i in range(3))
    by_sender[own_rows, :] = dot(win[own_rows, :], w_send[...]).astype(BF)
    by_receiver[...] = dot(win[own_rows, :], w_recv[...]).astype(BF)
    sums[...] = jnp.zeros_like(sums)
    for copy in small:
        copy.wait()
    get_up.wait()
    up_pre[...] = (
        dot(ub[...], w_edge[...])
        + b1[...]
        + dot_t(one_hot_t(count, up_send[...]), by_sender[own_rows, :])
    )
    get_down.wait()
    down_pre[...] = (
        dot(db[...], w_edge[...])
        + b1[...]
        + dot_t(one_hot_t(count, down_recv[...]), by_receiver[...])
    )
    blocks = TILE // 128
    index_rows = lambda t: pl.ds(pl.multiple_of(t * blocks, blocks), blocks)

    def main(t):
        get_edges(t).wait()
        pre[tile(t), :] = (
            dot(eb[tile(t), :], w_edge[...])
            + b1[...]
            + dot_t(one_hot_t(count, senders[index_rows(t), :] - RIM), by_sender[own_rows, :])
            + dot_t(one_hot_t(count, receivers[index_rows(t), :]), by_receiver[...])
        )

    def early_step(t, carry):
        main(t)
        return carry

    lax.fori_loop(0, early, early_step, 0)
    get_w2.wait()
    with jax.named_scope("wait_rim"):
        to_after.wait_recv()
        to_before.wait_recv()
    with jax.named_scope("wait_spread"):
        settle(table.at[all_but_one], spread_got)
    get_own.wait()
    table_over.start()
    by_sender[0:RIM, :] = dot(win[0:RIM, :], w_send[...]).astype(BF)
    by_sender[RIM + count :, :] = dot(win[RIM + count :, :], w_send[...]).astype(BF)

    @jax.named_scope("up")
    def up_stage():
        with jax.named_scope("wait_twin"):
            table_over.wait_recv()
        to_coarse = one_hot_t(2 * side, local_row(up_recv[...]))
        picked = dot_t(to_coarse, table[...]).astype(BF)
        new = tail(up_pre[...] + dot(picked, w_recv[...]), w2, b2, gain, shift)
        new = (ub[...].astype(F32) + new).astype(BF)
        ub[...] = new
        part[...] = dot(to_coarse, new).astype(BF)
        part_over.start()

    @jax.named_scope("home")
    def home_stage():
        with jax.named_scope("wait_part"):
            part_over.wait_recv()
        half[...] = (part[0:side, :].astype(F32) + beside[...].astype(F32)).astype(BF)
        landed[mine, :] = half[mine, :]

        def home(other, device):
            rows = pl.ds(pl.multiple_of(other * owned, owned), owned)
            remote(half.at[rows], landed.at[mine], home_sent, home_got, device).start()

        each_partner(home)

    def step(t, carry):
        base = pl.multiple_of(t * TILE, TILE)
        pl.when(t == 1)(up_stage)
        pl.when(t == 2)(home_stage)
        pl.when(t == early)(lambda: main(t))
        send_row = senders[index_rows(t), :]
        full = (
            pre[tile(t), :]
            + dot_t(one_hot_t(RIM, send_row), by_sender[0:RIM, :])
            + dot_t(one_hot_t(RIM, send_row - (RIM + count)), by_sender[RIM + count :, :])
        )
        wide = eb[tile(t), :].astype(F32)
        updated = wide + tail(full, w2, b2, gain, shift)
        alive = lax.broadcasted_iota(jnp.int32, updated.shape, 0) + base < live[0]
        sums[...] += dot(
            one_hot_t(count, receivers[index_rows(t), :]), jnp.where(alive, updated, 0.0).astype(BF)
        )
        eb[tile(t), :] = jnp.where(alive, updated, wide).astype(BF)
        return carry

    lax.fori_loop(0, steps, step, 0)

    with jax.named_scope("down"):
        picked = dot_t(one_hot_t(2 * side, local_row(down_send[...])), table[...]).astype(BF)
        new = tail(down_pre[...] + dot(picked, w_send[...]), w2, b2, gain, shift)
        new = (db[...].astype(F32) + new).astype(BF)
        db[...] = new
        total = (sums[...] + dot(one_hot_t(count, down_recv[...]), new)).astype(BF)
    get_v1.wait()
    get_v2.wait()

    def node_net(old, summed):
        inner = dot(old, v1[0:width, :]) + c1[...] + dot(summed, v1[width : 2 * width, :])
        return (old.astype(F32) + tail(inner, v2, c2, node_gain, node_shift)).astype(BF)

    with jax.named_scope("node"):
        fine_new[...] = node_net(win[own_rows, :], total)

    with jax.named_scope("wait_home"):
        settle(landed.at[all_but_one], home_got)
    with jax.named_scope("ends"):
        arrived = jnp.sum(landed[...].astype(F32).reshape(chips, owned, width), axis=0).astype(BF)
        coarse_new[...] = node_net(table[mine, :], arrived)
        to_after.wait_send()
        to_before.wait_send()
        settle(table.at[all_but_one], spread_sent)
        settle(half.at[all_but_one], home_sent)
        table_over.wait_send()
        part_over.wait_send()


def writer(fine, coarse, edges, up, down, *outs_and_sem):
    *outs, sem = outs_and_sem
    copies = []
    for source, target in zip((edges, fine, up, down, coarse), (outs[2], outs[0], *outs[3:], outs[1])):
        size = min(source.shape[0], 512)
        for at in range(0, source.shape[0], size):
            rows = pl.ds(at, size)
            copies.append(pltpu.make_async_copy(source.at[rows], target.at[rows], sem.at[len(copies)]))
    for copy in copies:
        copy.start()
    for copy in copies:
        copy.wait()


def body(
    fine_nodes, coarse_nodes, fine_edges, fine_senders, fine_receivers, fine_live,
    up_edges, up_senders, up_receivers, down_edges, down_senders, down_receivers,
    edge_in_weight, edge_in_bias, edge_out_weight, edge_out_bias, edge_gain, edge_shift,
    node_in_weight, node_in_bias, node_out_weight, node_out_bias, node_gain, node_shift,
):
    groups, patches = lax.axis_size("group"), lax.axis_size("patch")
    count, width = fine_nodes.shape
    owned = coarse_nodes.shape[0]
    slots = fine_edges.shape[0]
    crossing = up_edges.shape[0]
    everywhere = groups * patches * owned
    side = everywhere // 2
    steps = slots // TILE
    lanes = lambda index: index.reshape(-1, 128)
    row = lambda vector: vector.reshape(1, -1)
    vm = pl.BlockSpec(memory_space=pltpu.VMEM)
    anywhere = pl.BlockSpec(memory_space=pl.ANY)
    outs = (fine_nodes, coarse_nodes, fine_edges, up_edges, down_edges)
    rows = lambda n, dtype=BF: pltpu.VMEM((n, width), dtype)
    dma = pltpu.SemaphoreType.DMA
    indices = tuple(
        lanes(a)
        for a in (fine_senders, fine_receivers, up_senders, up_receivers, down_senders, down_receivers)
    )
    vectors = tuple(
        row(a)
        for a in (
            edge_in_bias, edge_out_bias, edge_gain, edge_shift,
            node_in_bias, node_out_bias, node_gain, node_shift,
        )
    )
    results = pl.pallas_call(
        functools.partial(kernel, groups, patches),
        out_shape=tuple(pltpu.VMEM(a.shape, a.dtype) for a in outs),
        in_specs=[pl.BlockSpec(memory_space=pltpu.SMEM)] + [anywhere] * 23,
        out_specs=(vm,) * 5,
        scratch_shapes=[
            rows(count + 2 * RIM),
            rows(3 * width), rows(width), rows(2 * width), rows(width),
            rows(count + 2 * RIM), rows(count), rows(slots, F32), rows(count, F32),
            rows(everywhere), rows(everywhere), rows(side), rows(side), rows(side),
            rows(crossing, F32), rows(crossing, F32),
            *(pltpu.VMEM(a.shape, a.dtype) for a in indices + vectors),
            dma((8 + steps,)), dma((len(indices + vectors),)), dma((2,)), dma((2,)),
            dma(()), dma(()), dma((2,)), dma((2,)), dma(()), dma(()),
        ],
        compiler_params=pltpu.CompilerParams(
            vmem_limit_bytes=50 * 1024 * 1024, collective_id=0, has_side_effects=True
        ),
    )(
        fine_live, *indices, *vectors,
        fine_nodes, coarse_nodes, fine_edges, up_edges, down_edges,
        edge_in_weight, edge_out_weight, node_in_weight, node_out_weight,
    )
    return pl.pallas_call(
        writer,
        out_shape=tuple(jax.ShapeDtypeStruct(a.shape, a.dtype) for a in outs),
        in_specs=[vm] * 5,
        out_specs=(anywhere,) * 5,
        scratch_shapes=[dma((slots // 512 + count // 512 + 3,))],
        compiler_params=pltpu.CompilerParams(vmem_limit_bytes=2**20),
    )(*results)


def solution(mesh):
    rows, vector = P(BOTH, None), P(BOTH)
    return jax.shard_map(
        body,
        mesh=mesh,
        in_specs=(rows,) * 3 + (vector,) * 3 + (rows, vector, vector) * 2 + (P(),) * 12,
        out_specs=(rows,) * 5,
        check_vma=False,
    )
```

time: 76.2 us -> 61 us (0.80)
  local copies, waits for them, and re-layouts: 9.74 us -> 0 us
  Pallas kernels: 64.9 us -> 59 us
    unnamed x9 -> x0, local copies, waits for them, and re-layouts: 9.74 us -> none
    pallas_call x1, Pallas kernels: 64.9 us -> 56.2 us  [body(): pl.pallas_call(functools.partial(kernel, groups, patches), out_shape=tupl...]
    pallas_call x0 -> x1, Pallas kernels: none -> 2.76 us  [body(): pl.pallas_call(writer, out_shape=tuple((jax.ShapeDtypeStruct(a.shape, a.d...]
where the time goes in v3:
time: 61 us; the launch traced here: 60.4 us
  Pallas kernels  59 us (97%)
  between operations  1.48 us (2%)
    pallas_call x1, Pallas kernels, body(): pl.pallas_call(functools.partial(kernel, groups, patches), out_shape=tupl...  56.2 us
    pallas_call x1, Pallas kernels, body(): pl.pallas_call(writer, out_shape=tuple((jax.ShapeDtypeStruct(a.shape, a.d...  2.76 us

profile of v3, /device:TPU:1, one launch (start us, length us, event | category | flops | bytes accessed | tf_op | source)
XLA Modules:
  0.0 60.4 jit_solution(16021927535346355343)
XLA Ops:
  1.3 56.2 %shard_map.263 = (bf16[1024,512]{1,0:T(8,128)(2,1)S(1)}, bf16[16,512]{1,0:T(8,128)(2,1)S(1)}, bf16[4096,512]{1,0:T(8,128)(2,1)S(1)}, bf16[512,512]{1,0:T(8,128)(2,1)S(1)}, bf16[512,512]{1,0:T(8,128)(2,1)S(1)}) custom-call(s32[1]{0:T(128)S(6)} %copy.29.live, s32[32,128]{1,0:T(8,128)} %bitcast.14, s32[32,128]{1,0:T(8,128)} %bitcast.15, s32[4,128]{1,0:T(4,128)} %bitcast.16, ...), custom_call_target="tpu_custom_call" | custom-call | tf_op jit(solution)/shard_map/pallas_call | solution.py:332
  57.5 2.8 %shard_map.264 = (bf16[1024,512]{1,0:T(8,128)(2,1)}, bf16[16,512]{1,0:T(8,128)(2,1)}, bf16[4096,512]{1,0:T(8,128)(2,1)}, bf16[512,512]{1,0:T(8,128)(2,1)}, bf16[512,512]{1,0:T(8,128)(2,1)}) custom-call(bf16[1024,512]{1,0:T(8,128)(2,1)S(1)} %get-tuple-element.10.fine, bf16[16,512]{1,0:T(8,128)(2,1)S(1)} %get-tuple-element.11.coarse, ...), custom_call_target="tpu_custom_call" | custom-call | tf_op jit(solution)/shard_map/pallas_call | solution.py:355

commit v4 on v3

--- a/solution.py
+++ b/solution.py
@@ -67,16 +67,26 @@
     chips = groups // 2 * patches
     side = chips * owned
     me = high * patches + p
+    planes = 4
+    plane = chips // planes
+    mine_y, mine_xz = me // plane, lax.rem(me, plane)
+    band = plane * owned
     twin = (high * 2 + 1 - core, p)
     mine = pl.ds(pl.multiple_of(me * owned, owned), owned)
 
-    def each_partner(action):
+    def in_plane(ahead, action):
+        y = lax.rem(mine_y + ahead, planes)
+
         def one(k, carry):
-            other = lax.rem(me + k, chips)
+            other = y * plane + lax.rem(mine_xz + k, plane)
             action(other, (other // patches * 2 + core, lax.rem(other, patches)))
             return carry
 
-        lax.fori_loop(1, chips, one, 0)
+        lax.fori_loop(0 if ahead else 1, plane, one, 0)
+
+    def ahead_rows(ahead, start=0):
+        y = lax.rem(mine_y + ahead + planes, planes)
+        return pl.ds(pl.multiple_of(y * band + start, band), band)
 
     def remote(source, target, sent, got, device):
         return pltpu.make_async_remote_copy(
@@ -92,7 +102,8 @@
         pl.semaphore_signal(barrier, inc=1, device_id=device, device_id_type=MESH)
 
     greet(0, twin)
-    each_partner(greet)
+    for ahead in range(planes):
+        in_plane(ahead, greet)
 
     steps = slots // TILE
     early = steps - 1
@@ -116,10 +127,48 @@
     small = [pltpu.make_async_copy(a, b, few.at[i]) for i, (a, b) in enumerate(small)]
     get_nodes.start()
     get_w1.start()
+    get_own.start()
+
+    before = (g, lax.rem(p + patches - 1, patches))
+    after = (g, lax.rem(p + 1, patches))
+    to_after = remote(
+        nodes.at[pl.ds(count - RIM, RIM)], win.at[pl.ds(0, RIM)], rim_sent.at[0], rim_got.at[0], after
+    )
+    to_before = remote(
+        nodes.at[pl.ds(0, RIM)], win.at[pl.ds(RIM + count, RIM)], rim_sent.at[1], rim_got.at[1], before
+    )
+    same = pl.ds(0, side)
+    other_side = pl.ds(side, side)
+    table_over = lambda ahead: remote(
+        table.at[ahead_rows(-ahead)],
+        table.at[ahead_rows(-ahead, side)],
+        twin_sent.at[ahead],
+        twin_got.at[ahead],
+        twin,
+    )
+    part_over = lambda ahead: remote(
+        part.at[ahead_rows(ahead, side)],
+        beside.at[ahead_rows(ahead)],
+        twin_sent.at[planes + ahead],
+        twin_got.at[planes + ahead],
+        twin,
+    )
+    all_but_one = pl.ds(0, side - owned)
+    arriving = lambda ahead: pl.ds(0, band if ahead else band - owned)
+
+    def spread(ahead):
+        def send(other, device):
+            remote(coarse, table.at[mine], spread_sent, spread_got.at[ahead], device).start()
+
+        in_plane(ahead, send)
+
+    with jax.named_scope("wait_bar"):
+        pl.semaphore_wait(barrier, chips)
+    for ahead in range(planes):
+        spread(ahead)
+    get_up.start()
     for copy in small:
         copy.start()
-    get_own.start()
-    get_up.start()
     get_down.start()
     for t in range(early):
         get_edges(t).start()
@@ -128,31 +177,6 @@
     get_v1.start()
     get_v2.start()
 
-    before = (g, lax.rem(p + patches - 1, patches))
-    after = (g, lax.rem(p + 1, patches))
-    to_after = remote(
-        nodes.at[pl.ds(count - RIM, RIM)], win.at[pl.ds(0, RIM)], rim_sent.at[0], rim_got.at[0], after
-    )
-    to_before = remote(
-        nodes.at[pl.ds(0, RIM)], win.at[pl.ds(RIM + count, RIM)], rim_sent.at[1], rim_got.at[1], before
-    )
-    same = pl.ds(0, side)
-    other_side = pl.ds(side, side)
-    table_over = remote(
-        table.at[same], table.at[other_side], twin_sent.at[0], twin_got.at[0], twin
-    )
-    part_over = remote(part.at[other_side], beside, twin_sent.at[1], twin_got.at[1], twin)
-    all_but_one = pl.ds(0, side - owned)
-
-    def spread(other, device):
-        remote(coarse, table.at[mine], spread_sent, spread_got, device).start()
-
-    with jax.named_scope("wait_bar"):
-        pl.semaphore_wait(barrier, chips)
-    each_partner(spread)
-    to_after.start()
-    to_before.start()
-
     def local_row(index):
         owner, inner = index // (patches * owned), lax.rem(index, patches * owned)
         away = jnp.where(lax.rem(owner, 2) == core, 0, side)
@@ -164,7 +188,6 @@
     w_edge, w_send, w_recv = (w1.at[pl.ds(i * width, width)] for i in range(3))
     by_sender[own_rows, :] = dot(win[own_rows, :], w_send[...]).astype(BF)
     by_receiver[...] = dot(win[own_rows, :], w_recv[...]).astype(BF)
-    sums[...] = jnp.zeros_like(sums)
     for copy in small:
         copy.wait()
     get_up.wait()
@@ -196,47 +219,57 @@
         return carry
 
     lax.fori_loop(0, early, early_step, 0)
+    get_own.wait()
+    for ahead in range(planes):
+        with jax.named_scope("wait_spread"):
+            settle(table.at[arriving(ahead)], spread_got.at[ahead])
+        table_over(ahead).start()
+    to_after.start()
+    to_before.start()
+    main(early)
     get_w2.wait()
-    with jax.named_scope("wait_rim"):
-        to_after.wait_recv()
-        to_before.wait_recv()
-    with jax.named_scope("wait_spread"):
-        settle(table.at[all_but_one], spread_got)
-    get_own.wait()
-    table_over.start()
-    by_sender[0:RIM, :] = dot(win[0:RIM, :], w_send[...]).astype(BF)
-    by_sender[RIM + count :, :] = dot(win[RIM + count :, :], w_send[...]).astype(BF)
-
-    @jax.named_scope("up")
-    def up_stage():
+
+    with jax.named_scope("up"):
         with jax.named_scope("wait_twin"):
-            table_over.wait_recv()
+            for ahead in range(planes):
+                table_over(ahead).wait_recv()
         to_coarse = one_hot_t(2 * side, local_row(up_recv[...]))
         picked = dot_t(to_coarse, table[...]).astype(BF)
         new = tail(up_pre[...] + dot(picked, w_recv[...]), w2, b2, gain, shift)
         new = (ub[...].astype(F32) + new).astype(BF)
         ub[...] = new
         part[...] = dot(to_coarse, new).astype(BF)
-        part_over.start()
-
-    @jax.named_scope("home")
-    def home_stage():
-        with jax.named_scope("wait_part"):
-            part_over.wait_recv()
-        half[...] = (part[0:side, :].astype(F32) + beside[...].astype(F32)).astype(BF)
+        for ahead in range(planes):
+            part_over(ahead).start()
+
+    with jax.named_scope("down"):
+        picked = dot_t(one_hot_t(2 * side, local_row(down_send[...])), table[...]).astype(BF)
+        new = tail(down_pre[...] + dot(picked, w_send[...]), w2, b2, gain, shift)
+        new = (db[...].astype(F32) + new).astype(BF)
+        db[...] = new
+        sums[...] = dot(one_hot_t(count, down_recv[...]), new)
+
+    with jax.named_scope("home"):
+        for ahead in range(planes):
+            part_over(ahead).wait_recv()
+            rows = ahead_rows(ahead)
+            half[rows, :] = (part[rows, :].astype(F32) + beside[rows, :].astype(F32)).astype(BF)
+
+            def home(other, device):
+                block = pl.ds(pl.multiple_of(other * owned, owned), owned)
+                remote(half.at[block], landed.at[mine], home_sent, home_got, device).start()
+
+            in_plane(ahead, home)
         landed[mine, :] = half[mine, :]
 
-        def home(other, device):
-            rows = pl.ds(pl.multiple_of(other * owned, owned), owned)
-            remote(half.at[rows], landed.at[mine], home_sent, home_got, device).start()
-
-        each_partner(home)
+    with jax.named_scope("wait_rim"):
+        to_after.wait_recv()
+        to_before.wait_recv()
+    by_sender[0:RIM, :] = dot(win[0:RIM, :], w_send[...]).astype(BF)
+    by_sender[RIM + count :, :] = dot(win[RIM + count :, :], w_send[...]).astype(BF)
 
     def step(t, carry):
         base = pl.multiple_of(t * TILE, TILE)
-        pl.when(t == 1)(up_stage)
-        pl.when(t == 2)(home_stage)
-        pl.when(t == early)(lambda: main(t))
         send_row = senders[index_rows(t), :]
         full = (
             pre[tile(t), :]
@@ -252,14 +285,8 @@
         eb[tile(t), :] = jnp.where(alive, updated, wide).astype(BF)
         return carry
 
-    lax.fori_loop(0, steps, step, 0)
-
-    with jax.named_scope("down"):
-        picked = dot_t(one_hot_t(2 * side, local_row(down_send[...])), table[...]).astype(BF)
-        new = tail(down_pre[...] + dot(picked, w_send[...]), w2, b2, gain, shift)
-        new = (db[...].astype(F32) + new).astype(BF)
-        db[...] = new
-        total = (sums[...] + dot(one_hot_t(count, down_recv[...]), new)).astype(BF)
+    with jax.named_scope("tails"):
+        lax.fori_loop(0, steps, step, 0)
     get_v1.wait()
     get_v2.wait()
 
@@ -268,7 +295,7 @@
         return (old.astype(F32) + tail(inner, v2, c2, node_gain, node_shift)).astype(BF)
 
     with jax.named_scope("node"):
-        fine_new[...] = node_net(win[own_rows, :], total)
+        fine_new[...] = node_net(win[own_rows, :], sums[...].astype(BF))
 
     with jax.named_scope("wait_home"):
         settle(landed.at[all_but_one], home_got)
@@ -279,8 +306,9 @@
         to_before.wait_send()
         settle(table.at[all_but_one], spread_sent)
         settle(half.at[all_but_one], home_sent)
-        table_over.wait_send()
-        part_over.wait_send()
+        for ahead in range(planes):
+            table_over(ahead).wait_send()
+            part_over(ahead).wait_send()
 
 
 def writer(fine, coarse, edges, up, down, *outs_and_sem):
@@ -342,7 +370,7 @@
             rows(crossing, F32), rows(crossing, F32),
             *(pltpu.VMEM(a.shape, a.dtype) for a in indices + vectors),
             dma((8 + steps,)), dma((len(indices + vectors),)), dma((2,)), dma((2,)),
-            dma(()), dma(()), dma((2,)), dma((2,)), dma(()), dma(()),
+            dma(()), dma((4,)), dma((8,)), dma((8,)), dma(()), dma(()),
         ],
         compiler_params=pltpu.CompilerParams(
             vmem_limit_bytes=50 * 1024 * 1024, collective_id=0, has_side_effects=True

time: 61 us -> 57.6 us (0.944)
  Pallas kernels: 59 us -> 55.7 us
    pallas_call x1, Pallas kernels: 56.2 us -> 52.9 us  [body(): pl.pallas_call(functools.partial(kernel, groups, patches), out_shape=tupl...]
where the time goes in v4:
time: 57.6 us; the launch traced here: 57.2 us
  Pallas kernels  55.7 us (97%)
  between operations  1.48 us (3%)
    pallas_call x1, Pallas kernels, body(): pl.pallas_call(functools.partial(kernel, groups, patches), out_shape=tupl...  52.9 us
    pallas_call x1, Pallas kernels, body(): pl.pallas_call(writer, out_shape=tuple((jax.ShapeDtypeStruct(a.shape, a.d...  2.76 us

profile of v4, /device:TPU:1, one launch (start us, length us, event | category | flops | bytes accessed | tf_op | source)
XLA Modules:
  0.0 57.2 jit_solution(5868127081196090782)
XLA Ops:
  1.3 52.9 %shard_map.263 = (bf16[1024,512]{1,0:T(8,128)(2,1)S(1)}, bf16[16,512]{1,0:T(8,128)(2,1)S(1)}, bf16[4096,512]{1,0:T(8,128)(2,1)S(1)}, bf16[512,512]{1,0:T(8,128)(2,1)S(1)}, bf16[512,512]{1,0:T(8,128)(2,1)S(1)}) custom-call(s32[1]{0:T(128)S(6)} %copy.29.live, s32[32,128]{1,0:T(8,128)} %bitcast.14, s32[32,128]{1,0:T(8,128)} %bitcast.15, s32[4,128]{1,0:T(4,128)} %bitcast.16, ...), custom_call_target="tpu_custom_call" | custom-call | tf_op jit(solution)/shard_map/pallas_call | solution.py:360
  54.2 2.8 %shard_map.264 = (bf16[1024,512]{1,0:T(8,128)(2,1)}, bf16[16,512]{1,0:T(8,128)(2,1)}, bf16[4096,512]{1,0:T(8,128)(2,1)}, bf16[512,512]{1,0:T(8,128)(2,1)}, bf16[512,512]{1,0:T(8,128)(2,1)}) custom-call(bf16[1024,512]{1,0:T(8,128)(2,1)S(1)} %get-tuple-element.10.fine, bf16[16,512]{1,0:T(8,128)(2,1)S(1)} %get-tuple-element.11.coarse, ...), custom_call_target="tpu_custom_call" | custom-call | tf_op jit(solution)/shard_map/pallas_call | solution.py:383

commit v5 on v4

--- a/solution.py
+++ b/solution.py
@@ -36,27 +36,28 @@
     return half + half * jnp.tanh(half)
 
 
-def normed(r, gain, shift):
-    centred = r - jnp.mean(r, axis=-1, keepdims=True)
-    spread = jnp.mean(centred * centred, axis=-1, keepdims=True)
-    return centred * lax.rsqrt(spread + 1e-05) * gain + shift
+def centred(matrix):
+    wide = matrix.astype(F32)
+    return (wide - jnp.mean(wide, axis=-1, keepdims=True)).astype(matrix.dtype)
 
 
 def tail(pre, out_weight, out_bias, gain, shift):
-    hidden = silu(pre).astype(BF)
-    return normed(dot(hidden, out_weight[...]) + out_bias[...], gain[...], shift[...])
+    r = dot(silu(pre).astype(BF), out_weight[...]) + out_bias[...]
+    spread = jnp.mean(r * r, axis=-1, keepdims=True)
+    return r * lax.rsqrt(spread + 1e-05) * gain[...] + shift[...]
 
 
 def kernel(
     groups, patches,
-    live, senders_in, receivers_in, up_send_in, up_recv_in, down_send_in, down_recv_in,
+    live_in, senders_in, receivers_in, up_send_in, up_recv_in, down_send_in, down_recv_in,
     b1_in, b2_in, gain_in, shift_in, c1_in, c2_in, node_gain_in, node_shift_in,
     nodes, coarse, edges, up, down, w1_in, w2_in, v1_in, v2_in,
     fine_new, coarse_new, eb, ub, db,
     win, w1, w2, v1, v2, by_sender, by_receiver, pre, sums, table, part, beside, half,
-    landed, up_pre, down_pre,
+    landed, up_pre,
     senders, receivers, up_send, up_recv, down_send, down_recv,
     b1, b2, gain, shift, c1, c2, node_gain, node_shift,
+    by_rim, live,
     load, few, rim_sent, rim_got, spread_sent, spread_got, twin_sent, twin_got, home_sent, home_got,
 ):
     count, width = nodes.shape
@@ -76,13 +77,15 @@
 
     def in_plane(ahead, action):
         y = lax.rem(mine_y + ahead, planes)
+        group = y * plane // patches * 2 + core
+        first = lax.rem(y * plane, patches)
 
         def one(k, carry):
-            other = y * plane + lax.rem(mine_xz + k, plane)
-            action(other, (other // patches * 2 + core, lax.rem(other, patches)))
+            action(y * plane + k, (group, first + k))
             return carry
 
-        lax.fori_loop(0 if ahead else 1, plane, one, 0)
+        lax.fori_loop(mine_xz if ahead else mine_xz + 1, plane, one, 0)
+        lax.fori_loop(0, mine_xz, one, 0)
 
     def ahead_rows(ahead, start=0):
         y = lax.rem(mine_y + ahead + planes, planes)
@@ -119,7 +122,7 @@
     get_v2 = pltpu.make_async_copy(v2_in, v2, load.at[7])
     get_edges = lambda t: pltpu.make_async_copy(edges.at[tile(t)], eb.at[tile(t)], load.at[8 + t])
     small = (
-        (senders_in, senders), (receivers_in, receivers), (up_send_in, up_send),
+        (live_in, live), (senders_in, senders), (receivers_in, receivers), (up_send_in, up_send),
         (up_recv_in, up_recv), (down_send_in, down_send), (down_recv_in, down_recv),
         (b1_in, b1), (b2_in, b2), (gain_in, gain), (shift_in, shift), (c1_in, c1), (c2_in, c2),
         (node_gain_in, node_gain), (node_shift_in, node_shift),
@@ -186,7 +189,7 @@
         get_nodes.wait()
         get_w1.wait()
     w_edge, w_send, w_recv = (w1.at[pl.ds(i * width, width)] for i in range(3))
-    by_sender[own_rows, :] = dot(win[own_rows, :], w_send[...]).astype(BF)
+    by_sender[...] = dot(win[own_rows, :], w_send[...]).astype(BF)
     by_receiver[...] = dot(win[own_rows, :], w_recv[...]).astype(BF)
     for copy in small:
         copy.wait()
@@ -194,13 +197,7 @@
     up_pre[...] = (
         dot(ub[...], w_edge[...])
         + b1[...]
-        + dot_t(one_hot_t(count, up_send[...]), by_sender[own_rows, :])
-    )
-    get_down.wait()
-    down_pre[...] = (
-        dot(db[...], w_edge[...])
-        + b1[...]
-        + dot_t(one_hot_t(count, down_recv[...]), by_receiver[...])
+        + dot_t(one_hot_t(count, up_send[...]), by_sender[...])
     )
     blocks = TILE // 128
     index_rows = lambda t: pl.ds(pl.multiple_of(t * blocks, blocks), blocks)
@@ -210,7 +207,7 @@
         pre[tile(t), :] = (
             dot(eb[tile(t), :], w_edge[...])
             + b1[...]
-            + dot_t(one_hot_t(count, senders[index_rows(t), :] - RIM), by_sender[own_rows, :])
+            + dot_t(one_hot_t(count, senders[index_rows(t), :] - RIM), by_sender[...])
             + dot_t(one_hot_t(count, receivers[index_rows(t), :]), by_receiver[...])
         )
 
@@ -218,36 +215,38 @@
         main(t)
         return carry
 
-    lax.fori_loop(0, early, early_step, 0)
-    get_own.wait()
-    for ahead in range(planes):
+    def pass_on(ahead):
         with jax.named_scope("wait_spread"):
             settle(table.at[arriving(ahead)], spread_got.at[ahead])
         table_over(ahead).start()
+
+    lax.fori_loop(0, early, early_step, 0)
+    get_own.wait()
+    get_w2.wait()
+    pass_on(0)
+    pass_on(1)
+    main(early)
+    w2[...] = centred(w2[...])
+    b2[...] = centred(b2[...])
+    pass_on(2)
+    pass_on(3)
     to_after.start()
     to_before.start()
-    main(early)
-    get_w2.wait()
-
+    near, far = slice(0, side), slice(side, 2 * side)
     with jax.named_scope("up"):
+        to_coarse = one_hot_t(2 * side, local_row(up_recv[...]))
+        picked = dot_t(to_coarse[near], table[near, :])
         with jax.named_scope("wait_twin"):
             for ahead in range(planes):
                 table_over(ahead).wait_recv()
-        to_coarse = one_hot_t(2 * side, local_row(up_recv[...]))
-        picked = dot_t(to_coarse, table[...]).astype(BF)
+        picked = (picked + dot_t(to_coarse[far], table[far, :])).astype(BF)
         new = tail(up_pre[...] + dot(picked, w_recv[...]), w2, b2, gain, shift)
         new = (ub[...].astype(F32) + new).astype(BF)
         ub[...] = new
-        part[...] = dot(to_coarse, new).astype(BF)
+        part[far, :] = dot(to_coarse[far], new).astype(BF)
         for ahead in range(planes):
             part_over(ahead).start()
-
-    with jax.named_scope("down"):
-        picked = dot_t(one_hot_t(2 * side, local_row(down_send[...])), table[...]).astype(BF)
-        new = tail(down_pre[...] + dot(picked, w_send[...]), w2, b2, gain, shift)
-        new = (db[...].astype(F32) + new).astype(BF)
-        db[...] = new
-        sums[...] = dot(one_hot_t(count, down_recv[...]), new)
+        part[near, :] = dot(to_coarse[near], new).astype(BF)
 
     with jax.named_scope("home"):
         for ahead in range(planes):
@@ -262,33 +261,61 @@
             in_plane(ahead, home)
         landed[mine, :] = half[mine, :]
 
+    with jax.named_scope("down"):
+        get_down.wait()
+        picked = dot_t(one_hot_t(2 * side, local_row(down_send[...])), table[...]).astype(BF)
+        to_fine = one_hot_t(count, down_recv[...])
+        full = (
+            dot(db[...], w_edge[...])
+            + b1[...]
+            + dot_t(to_fine, by_receiver[...])
+            + dot(picked, w_send[...])
+        )
+        new = tail(full, w2, b2, gain, shift)
+        new = (db[...].astype(F32) + new).astype(BF)
+        db[...] = new
+        sums[...] = dot(to_fine, new)
+
     with jax.named_scope("wait_rim"):
         to_after.wait_recv()
         to_before.wait_recv()
-    by_sender[0:RIM, :] = dot(win[0:RIM, :], w_send[...]).astype(BF)
-    by_sender[RIM + count :, :] = dot(win[RIM + count :, :], w_send[...]).astype(BF)
-
-    def step(t, carry):
-        base = pl.multiple_of(t * TILE, TILE)
+    by_rim[0:RIM, :] = dot(win[0:RIM, :], w_send[...]).astype(BF)
+    by_rim[RIM:, :] = dot(win[RIM + count :, :], w_send[...]).astype(BF)
+
+    def finished(t):
         send_row = senders[index_rows(t), :]
-        full = (
-            pre[tile(t), :]
-            + dot_t(one_hot_t(RIM, send_row), by_sender[0:RIM, :])
-            + dot_t(one_hot_t(RIM, send_row - (RIM + count)), by_sender[RIM + count :, :])
-        )
-        wide = eb[tile(t), :].astype(F32)
-        updated = wide + tail(full, w2, b2, gain, shift)
-        alive = lax.broadcasted_iota(jnp.int32, updated.shape, 0) + base < live[0]
+        rim_row = jnp.where(
+            send_row < RIM, send_row, jnp.where(send_row < RIM + count, -1, send_row - count)
+        )
+        new = tail(
+            pre[tile(t), :] + dot_t(one_hot_t(2 * RIM, rim_row), by_rim[...]), w2, b2, gain, shift
+        )
+        slot = lax.broadcasted_iota(jnp.int32, (TILE, 1), 0) + t * TILE
+        return (eb[tile(t), :].astype(F32) + jnp.where(slot < live[0], new, 0.0)).astype(BF)
+
+    def step(i, carry):
+        first, second = finished(2 * i), finished(2 * i + 1)
+        eb[tile(2 * i), :] = first
+        eb[tile(2 * i + 1), :] = second
+        rows = pl.ds(pl.multiple_of(2 * i * blocks, 2 * blocks), 2 * blocks)
+        index = receivers[rows, :]
+        slot = (
+            lax.broadcasted_iota(jnp.int32, index.shape, 0) * 128
+            + lax.broadcasted_iota(jnp.int32, index.shape, 1)
+            + 2 * i * TILE
+        )
         sums[...] += dot(
-            one_hot_t(count, receivers[index_rows(t), :]), jnp.where(alive, updated, 0.0).astype(BF)
-        )
-        eb[tile(t), :] = jnp.where(alive, updated, wide).astype(BF)
+            one_hot_t(count, jnp.where(slot < live[0], index, -1)),
+            jnp.concatenate([first, second], axis=0),
+        )
         return carry
 
     with jax.named_scope("tails"):
-        lax.fori_loop(0, steps, step, 0)
+        lax.fori_loop(0, steps // 2, step, 0)
     get_v1.wait()
     get_v2.wait()
+    v2[...] = centred(v2[...])
+    c2[...] = centred(c2[...])
 
     def node_net(old, summed):
         inner = dot(old, v1[0:width, :]) + c1[...] + dot(summed, v1[width : 2 * width, :])
@@ -360,16 +387,17 @@
     results = pl.pallas_call(
         functools.partial(kernel, groups, patches),
         out_shape=tuple(pltpu.VMEM(a.shape, a.dtype) for a in outs),
-        in_specs=[pl.BlockSpec(memory_space=pltpu.SMEM)] + [anywhere] * 23,
+        in_specs=[anywhere] * 24,
         out_specs=(vm,) * 5,
         scratch_shapes=[
             rows(count + 2 * RIM),
             rows(3 * width), rows(width), rows(2 * width), rows(width),
-            rows(count + 2 * RIM), rows(count), rows(slots, F32), rows(count, F32),
+            rows(count), rows(count), rows(slots, F32), rows(count, F32),
             rows(everywhere), rows(everywhere), rows(side), rows(side), rows(side),
-            rows(crossing, F32), rows(crossing, F32),
+            rows(crossing, F32),
             *(pltpu.VMEM(a.shape, a.dtype) for a in indices + vectors),
-            dma((8 + steps,)), dma((len(indices + vectors),)), dma((2,)), dma((2,)),
+            rows(2 * RIM), pltpu.SMEM((1,), jnp.int32),
+            dma((8 + steps,)), dma((len(indices + vectors) + 1,)), dma((2,)), dma((2,)),
             dma(()), dma((4,)), dma((8,)), dma((8,)), dma(()), dma(()),
         ],
         compiler_params=pltpu.CompilerParams(

time: 57.6 us -> 54.9 us (0.953)
  Pallas kernels: 55.7 us -> 53.3 us
    pallas_call x1, Pallas kernels: 52.9 us -> 50.6 us  [body(): pl.pallas_call(functools.partial(kernel, groups, patches), out_shape=tupl...]
where the time goes in v5:
time: 54.9 us; the launch traced here: 54.8 us
  Pallas kernels  53.3 us (97%)
  between operations  1.46 us (3%)
    pallas_call x1, Pallas kernels, body(): pl.pallas_call(functools.partial(kernel, groups, patches), out_shape=tupl...  50.6 us
    pallas_call x1, Pallas kernels, body(): pl.pallas_call(writer, out_shape=tuple((jax.ShapeDtypeStruct(a.shape, a.d...  2.76 us

profile of v5, /device:TPU:1, one launch (start us, length us, event | category | flops | bytes accessed | tf_op | source)
XLA Modules:
  0.0 54.8 jit_solution(8069605629275190044)
XLA Ops:
  1.3 50.6 %shard_map.263 = (bf16[1024,512]{1,0:T(8,128)(2,1)S(1)}, bf16[16,512]{1,0:T(8,128)(2,1)S(1)}, bf16[4096,512]{1,0:T(8,128)(2,1)S(1)}, bf16[512,512]{1,0:T(8,128)(2,1)S(1)}, bf16[512,512]{1,0:T(8,128)(2,1)S(1)}) custom-call(s32[1]{0:T(128)S(6)} %copy.29.live_in, s32[32,128]{1,0:T(8,128)} %bitcast.14, s32[32,128]{1,0:T(8,128)} %bitcast.15, s32[4,128]{1,0:T(4,128)} %bitcast.16, ...), custom_call_target="tpu_custom_call" | custom-call | tf_op jit(solution)/shard_map/pallas_call | solution.py:387
  51.9 2.8 %shard_map.264 = (bf16[1024,512]{1,0:T(8,128)(2,1)}, bf16[16,512]{1,0:T(8,128)(2,1)}, bf16[4096,512]{1,0:T(8,128)(2,1)}, bf16[512,512]{1,0:T(8,128)(2,1)}, bf16[512,512]{1,0:T(8,128)(2,1)}) custom-call(bf16[1024,512]{1,0:T(8,128)(2,1)S(1)} %get-tuple-element.10.fine, bf16[16,512]{1,0:T(8,128)(2,1)S(1)} %get-tuple-element.11.coarse, ...), custom_call_target="tpu_custom_call" | custom-call | tf_op jit(solution)/shard_map/pallas_call | solution.py:411

commit v6 on v5

--- a/solution.py
+++ b/solution.py
@@ -54,7 +54,7 @@
     nodes, coarse, edges, up, down, w1_in, w2_in, v1_in, v2_in,
     fine_new, coarse_new, eb, ub, db,
     win, w1, w2, v1, v2, by_sender, by_receiver, pre, sums, table, part, beside, half,
-    landed, up_pre,
+    landed, up_pre, down_pre,
     senders, receivers, up_send, up_recv, down_send, down_recv,
     b1, b2, gain, shift, c1, c2, node_gain, node_shift,
     by_rim, live,
@@ -161,14 +161,13 @@
 
     def spread(ahead):
         def send(other, device):
-            remote(coarse, table.at[mine], spread_sent, spread_got.at[ahead], device).start()
+            remote(table.at[mine], table.at[mine], spread_sent, spread_got.at[ahead], device).start()
 
         in_plane(ahead, send)
 
-    with jax.named_scope("wait_bar"):
-        pl.semaphore_wait(barrier, chips)
-    for ahead in range(planes):
-        spread(ahead)
+    with jax.named_scope("wait_load"):
+        get_nodes.wait()
+        get_w1.wait()
     get_up.start()
     for copy in small:
         copy.start()
@@ -179,18 +178,20 @@
     get_edges(early).start()
     get_v1.start()
     get_v2.start()
+    w_edge, w_send, w_recv = (w1.at[pl.ds(i * width, width)] for i in range(3))
+    by_sender[...] = dot(win[own_rows, :], w_send[...]).astype(BF)
+    by_receiver[...] = dot(win[own_rows, :], w_recv[...]).astype(BF)
+    get_own.wait()
+    with jax.named_scope("wait_bar"):
+        pl.semaphore_wait(barrier, chips)
+    for ahead in range(planes):
+        spread(ahead)
 
     def local_row(index):
         owner, inner = index // (patches * owned), lax.rem(index, patches * owned)
         away = jnp.where(lax.rem(owner, 2) == core, 0, side)
         return owner // 2 * (patches * owned) + inner + away
 
-    with jax.named_scope("wait_load"):
-        get_nodes.wait()
-        get_w1.wait()
-    w_edge, w_send, w_recv = (w1.at[pl.ds(i * width, width)] for i in range(3))
-    by_sender[...] = dot(win[own_rows, :], w_send[...]).astype(BF)
-    by_receiver[...] = dot(win[own_rows, :], w_recv[...]).astype(BF)
     for copy in small:
         copy.wait()
     get_up.wait()
@@ -221,7 +222,6 @@
         table_over(ahead).start()
 
     lax.fori_loop(0, early, early_step, 0)
-    get_own.wait()
     get_w2.wait()
     pass_on(0)
     pass_on(1)
@@ -232,6 +232,12 @@
     pass_on(3)
     to_after.start()
     to_before.start()
+    get_down.wait()
+    down_pre[...] = (
+        dot(db[...], w_edge[...])
+        + b1[...]
+        + dot_t(one_hot_t(count, down_recv[...]), by_receiver[...])
+    )
     near, far = slice(0, side), slice(side, 2 * side)
     with jax.named_scope("up"):
         to_coarse = one_hot_t(2 * side, local_row(up_recv[...]))
@@ -262,16 +268,9 @@
         landed[mine, :] = half[mine, :]
 
     with jax.named_scope("down"):
-        get_down.wait()
         picked = dot_t(one_hot_t(2 * side, local_row(down_send[...])), table[...]).astype(BF)
         to_fine = one_hot_t(count, down_recv[...])
-        full = (
-            dot(db[...], w_edge[...])
-            + b1[...]
-            + dot_t(to_fine, by_receiver[...])
-            + dot(picked, w_send[...])
-        )
-        new = tail(full, w2, b2, gain, shift)
+        new = tail(down_pre[...] + dot(picked, w_send[...]), w2, b2, gain, shift)
         new = (db[...].astype(F32) + new).astype(BF)
         db[...] = new
         sums[...] = dot(to_fine, new)
@@ -394,7 +393,7 @@
             rows(3 * width), rows(width), rows(2 * width), rows(width),
             rows(count), rows(count), rows(slots, F32), rows(count, F32),
             rows(everywhere), rows(everywhere), rows(side), rows(side), rows(side),
-            rows(crossing, F32),
+            rows(crossing, F32), rows(crossing, F32),
             *(pltpu.VMEM(a.shape, a.dtype) for a in indices + vectors),
             rows(2 * RIM), pltpu.SMEM((1,), jnp.int32),
             dma((8 + steps,)), dma((len(indices + vectors) + 1,)), dma((2,)), dma((2,)),

time: 54.9 us -> 55.4 us (level)
  no operation moved by 1% of the time
where the time goes in v6:
time: 55.4 us; the launch traced here: 55.3 us
  Pallas kernels  53.8 us (97%)
  between operations  1.46 us (3%)
    pallas_call x1, Pallas kernels, body(): pl.pallas_call(functools.partial(kernel, groups, patches), out_shape=tupl...  51.1 us
    pallas_call x1, Pallas kernels, body(): pl.pallas_call(writer, out_shape=tuple((jax.ShapeDtypeStruct(a.shape, a.d...  2.76 us

profile of v6, /device:TPU:1, one launch (start us, length us, event | category | flops | bytes accessed | tf_op | source)
XLA Modules:
  0.0 55.3 jit_solution(15661789438361797016)
XLA Ops:
  1.3 51.1 %shard_map.263 = (bf16[1024,512]{1,0:T(8,128)(2,1)S(1)}, bf16[16,512]{1,0:T(8,128)(2,1)S(1)}, bf16[4096,512]{1,0:T(8,128)(2,1)S(1)}, bf16[512,512]{1,0:T(8,128)(2,1)S(1)}, bf16[512,512]{1,0:T(8,128)(2,1)S(1)}) custom-call(s32[1]{0:T(128)S(6)} %copy.29.live_in, s32[32,128]{1,0:T(8,128)} %bitcast.14, s32[32,128]{1,0:T(8,128)} %bitcast.15, s32[4,128]{1,0:T(4,128)} %bitcast.16, ...), custom_call_target="tpu_custom_call" | custom-call | tf_op jit(solution)/shard_map/pallas_call | solution.py:386
  52.3 2.8 %shard_map.264 = (bf16[1024,512]{1,0:T(8,128)(2,1)}, bf16[16,512]{1,0:T(8,128)(2,1)}, bf16[4096,512]{1,0:T(8,128)(2,1)}, bf16[512,512]{1,0:T(8,128)(2,1)}, bf16[512,512]{1,0:T(8,128)(2,1)}) custom-call(bf16[1024,512]{1,0:T(8,128)(2,1)S(1)} %get-tuple-element.10.fine, bf16[16,512]{1,0:T(8,128)(2,1)S(1)} %get-tuple-element.11.coarse, ...), custom_call_target="tpu_custom_call" | custom-call | tf_op jit(solution)/shard_map/pallas_call | solution.py:410

commit v7 on v5

--- a/solution.py
+++ b/solution.py
@@ -161,10 +161,11 @@
 
     def spread(ahead):
         def send(other, device):
-            remote(coarse, table.at[mine], spread_sent, spread_got.at[ahead], device).start()
+            remote(table.at[mine], table.at[mine], spread_sent, spread_got.at[ahead], device).start()
 
         in_plane(ahead, send)
 
+    get_own.wait()
     with jax.named_scope("wait_bar"):
         pl.semaphore_wait(barrier, chips)
     for ahead in range(planes):
@@ -221,7 +222,6 @@
         table_over(ahead).start()
 
     lax.fori_loop(0, early, early_step, 0)
-    get_own.wait()
     get_w2.wait()
     pass_on(0)
     pass_on(1)
@@ -230,8 +230,6 @@
     b2[...] = centred(b2[...])
     pass_on(2)
     pass_on(3)
-    to_after.start()
-    to_before.start()
     near, far = slice(0, side), slice(side, 2 * side)
     with jax.named_scope("up"):
         to_coarse = one_hot_t(2 * side, local_row(up_recv[...]))
@@ -239,6 +237,8 @@
         with jax.named_scope("wait_twin"):
             for ahead in range(planes):
                 table_over(ahead).wait_recv()
+        to_after.start()
+        to_before.start()
         picked = (picked + dot_t(to_coarse[far], table[far, :])).astype(BF)
         new = tail(up_pre[...] + dot(picked, w_recv[...]), w2, b2, gain, shift)
         new = (ub[...].astype(F32) + new).astype(BF)

time: 54.9 us -> 54.9 us (level)
  no operation moved by 1% of the time
where the time goes in v7:
time: 54.9 us; the launch traced here: 54.8 us
  Pallas kernels  53.3 us (97%)
  between operations  1.46 us (3%)
    pallas_call x1, Pallas kernels, body(): pl.pallas_call(functools.partial(kernel, groups, patches), out_shape=tupl...  50.5 us
    pallas_call x1, Pallas kernels, body(): pl.pallas_call(writer, out_shape=tuple((jax.ShapeDtypeStruct(a.shape, a.d...  2.76 us

profile of v7, /device:TPU:1, one launch (start us, length us, event | category | flops | bytes accessed | tf_op | source)
XLA Modules:
  0.0 54.8 jit_solution(11532630522643245937)
XLA Ops:
  1.3 50.5 %shard_map.263 = (bf16[1024,512]{1,0:T(8,128)(2,1)S(1)}, bf16[16,512]{1,0:T(8,128)(2,1)S(1)}, bf16[4096,512]{1,0:T(8,128)(2,1)S(1)}, bf16[512,512]{1,0:T(8,128)(2,1)S(1)}, bf16[512,512]{1,0:T(8,128)(2,1)S(1)}) custom-call(s32[1]{0:T(128)S(6)} %copy.29.live_in, s32[32,128]{1,0:T(8,128)} %bitcast.14, s32[32,128]{1,0:T(8,128)} %bitcast.15, s32[4,128]{1,0:T(4,128)} %bitcast.16, ...), custom_call_target="tpu_custom_call" | custom-call | tf_op jit(solution)/shard_map/pallas_call | solution.py:387
  51.8 2.8 %shard_map.264 = (bf16[1024,512]{1,0:T(8,128)(2,1)}, bf16[16,512]{1,0:T(8,128)(2,1)}, bf16[4096,512]{1,0:T(8,128)(2,1)}, bf16[512,512]{1,0:T(8,128)(2,1)}, bf16[512,512]{1,0:T(8,128)(2,1)}) custom-call(bf16[1024,512]{1,0:T(8,128)(2,1)S(1)} %get-tuple-element.10.fine, bf16[16,512]{1,0:T(8,128)(2,1)S(1)} %get-tuple-element.11.coarse, ...), custom_call_target="tpu_custom_call" | custom-call | tf_op jit(solution)/shard_map/pallas_call | solution.py:411
